TPU v7x, 32 devices: a whole 2x2x4 slice. The times are simulated.
32 devices in a mesh: tp: 4 (over z), dp: 8 (over y, x, core).
Axes of the slice: x: 2, y: 2, z: 4, core: 2. Of those that a mesh axis runs over, the one named last changes fastest.
Arguments:
- hidden_in: bfloat16 [16384, 1024], P('dp')
- targets: bfloat16 [16384, 1024], P('dp')
- w_up: bfloat16 [4, 1024, 4096], P(None, None, 'tp')
- w_down: bfloat16 [4, 4096, 1024], P(None, 'tp')
Outputs:
- output 1: float32 [4, 1024, 4096], P(None, None, 'tp')
- output 2: float32 [4, 4096, 1024], P(None, 'tp')
All inputs are finite; a program needn't handle non-finite values.
Results may differ from a plain program's by a relative error of at most 0.0103568.
Values are sent between devices in bfloat16 or wider.
A program may use at most 1 GiB of HBM per device.

v0:
```python
import functools
import jax
import jax.numpy as jnp
from jax import lax
from jax.sharding import PartitionSpec as P

ROW_CONTRACT = (((0,), (0,)), ((), ()))
COL_CONTRACT = (((1,), (1,)), ((), ()))


def gelu_tanh(value):
    return jax.nn.gelu(value, approximate=True)


def local_step(hidden, targets, w_up, w_down, total_tokens):
    layers = w_up.shape[0]
    h_cur = hidden
    saved = []
    for layer in range(layers):
        pre_act = jnp.dot(h_cur, w_up[layer], preferred_element_type=jnp.float32).astype(jnp.bfloat16)
        act_val = gelu_tanh(pre_act.astype(jnp.float32)).astype(jnp.bfloat16)
        part_out = jnp.dot(act_val, w_down[layer], preferred_element_type=jnp.float32)
        branch = lax.psum(part_out, "tp").astype(jnp.bfloat16)
        saved.append((h_cur, pre_act, act_val))
        h_cur = h_cur + branch
    err_f32 = (h_cur.astype(jnp.float32) - targets.astype(jnp.float32)) / total_tokens
    g_cur = err_f32.astype(jnp.bfloat16)
    grads_up = [None] * layers
    grads_down = [None] * layers
    for layer in reversed(range(layers)):
        h_in, pre_act, act_val = saved[layer]
        g_down = lax.dot_general(act_val, g_cur, ROW_CONTRACT, preferred_element_type=jnp.float32)
        grads_down[layer] = lax.psum(g_down, "dp")
        d_act = lax.dot_general(g_cur, w_down[layer], COL_CONTRACT, preferred_element_type=jnp.float32)
        _, gelu_vjp = jax.vjp(gelu_tanh, pre_act.astype(jnp.float32))
        d_pre = gelu_vjp(d_act)[0].astype(jnp.bfloat16)
        g_up = lax.dot_general(h_in, d_pre, ROW_CONTRACT, preferred_element_type=jnp.float32)
        grads_up[layer] = lax.psum(g_up, "dp")
        if layer > 0:
            back_part = lax.dot_general(d_pre, w_up[layer], COL_CONTRACT, preferred_element_type=jnp.float32)
            g_cur = (g_cur.astype(jnp.float32) + lax.psum(back_part, "tp")).astype(jnp.bfloat16)
    return jnp.stack(grads_up), jnp.stack(grads_down)


def solution(mesh):
    def grad_step(hidden_in, targets, w_up, w_down):
        step_fn = functools.partial(local_step, total_tokens=hidden_in.shape[0])
        mapped = jax.shard_map(step_fn, mesh=mesh, in_specs=(P("dp", None), P("dp", None), P(None, None, "tp"), P(None, "tp", None)), out_specs=(P(None, None, "tp"), P(None, "tp", None)), check_vma=False)
        return mapped(hidden_in, targets, w_up, w_down)

    return grad_step
```

profile of v0, /device:TPU:0, one launch (start us, length us, event | category | flops | bytes accessed | tf_op | source)
XLA Modules:
  0.0 2657.0 jit_solution(5429427120041075925)
XLA Ops:
  7.2 7.4 convolution_convert_fusion.3
  14.6 2.0 copy-done.11
  16.6 9.1 fusion.74
  25.7 286.2 %all-reduce.17 = bf16[2048,1024]{1,0:T(8,128)(2,1)} all-reduce(f32[2048,1024]{1,0:T(8,128)} %fusion.74), channel_id=1, replica_groups=mesh['tp'=4,'dp'=8] {'tp'}, use_global_device_ids=true, to_apply=%region_0.0 | all-reduce | flops 2097152 | bytes 12582912 | tf_op jit(solution)/shard_map/psum | solution.py:23
  311.9 5.6 add.180
  317.5 7.8 convolution_convert_fusion.2
  325.4 1.9 copy-done.12
  327.3 9.1 fusion.65
  336.5 279.6 %all-reduce.18 = bf16[2048,1024]{1,0:T(8,128)(2,1)} all-reduce(f32[2048,1024]{1,0:T(8,128)} %fusion.65), channel_id=1, replica_groups=mesh['tp'=4,'dp'=8] {'tp'}, use_global_device_ids=true, to_apply=%region_1.0 | all-reduce | flops 2097152 | bytes 12582912 | tf_op jit(solution)/shard_map/psum | solution.py:23
  616.0 5.6 add.179
  621.6 7.9 convolution_convert_fusion.1
  629.5 2.0 copy-done.15
  631.4 9.1 fusion.56
  640.6 278.4 %all-reduce.19 = bf16[2048,1024]{1,0:T(8,128)(2,1)} all-reduce(f32[2048,1024]{1,0:T(8,128)} %fusion.56), channel_id=1, replica_groups=mesh['tp'=4,'dp'=8] {'tp'}, use_global_device_ids=true, to_apply=%region_2.0 | all-reduce | flops 2097152 | bytes 12582912 | tf_op jit(solution)/shard_map/psum | solution.py:23
  918.9 5.6 add.178
  924.5 7.9 convolution_convert_fusion
  932.4 1.9 copy-done.18
  934.3 9.1 fusion.47
  943.5 277.2 %all-reduce.20 = bf16[2048,1024]{1,0:T(8,128)(2,1)} all-reduce(f32[2048,1024]{1,0:T(8,128)} %fusion.47), channel_id=1, replica_groups=mesh['tp'=4,'dp'=8] {'tp'}, use_global_device_ids=true, to_apply=%region_3.0 | all-reduce | flops 2097152 | bytes 12582912 | tf_op jit(solution)/shard_map/psum | solution.py:23
  1220.7 8.0 multiply_convert_fusion
  1228.7 12.0 fusion.6
  1240.8 1.9 copy-done.21
  1242.7 8.4 fusion.51
  1251.1 0.3 all-reduce.12.cloned.1.call-start
  1251.4 290.6 %all-reduce.10.cloned.1.call-done = f32[2048,1024]{1,0:T(8,128)} async-done(((f32[2048,1024]{1,0:T(8,128)}), f32[2048,1024]{1,0:T(8,128)}) %all-reduce.10.cloned.1.call-update) | async-done | bytes 8388624 | tf_op jit(solution)/shard_map/psum | solution.py:41
  1542.0 6.4 add_convert_fusion.2
  1548.3 12.0 fusion.9
  1560.4 2.0 copy-done.22
  1562.4 8.4 fusion.60
  1570.7 0.4 all-reduce.14.cloned.1.call-start
  1571.2 287.4 %all-reduce.12.cloned.1.call-done = f32[2048,1024]{1,0:T(8,128)} async-done(((f32[2048,1024]{1,0:T(8,128)}), f32[2048,1024]{1,0:T(8,128)}) %all-reduce.12.cloned.1.call-update) | async-done | bytes 8388624 | tf_op jit(solution)/shard_map/psum | solution.py:41
  1858.6 6.4 add_convert_fusion.1
  1865.0 12.0 fusion.12
  1877.0 2.0 copy-done.24
  1879.1 8.3 fusion.69
  1887.5 10.2 convolution_bitcast_fusion.4
  1897.7 6.6 convolution_bitcast_fusion
  1904.3 6.2 convolution_bitcast_fusion.5
  1910.5 6.5 convolution_bitcast_fusion.1
  1917.0 6.2 convolution_bitcast_fusion.6
  1923.2 6.6 convolution_bitcast_fusion.2
  1929.8 245.5 %all-reduce.14.cloned.1.call-done = f32[2048,1024]{1,0:T(8,128)} async-done(((f32[2048,1024]{1,0:T(8,128)}), f32[2048,1024]{1,0:T(8,128)}) %all-reduce.14.cloned.1.call-update) | async-done | bytes 8388624 | tf_op jit(solution)/shard_map/psum | solution.py:41
  2175.3 14.2 convolution_bitcast_fusion.3
  2189.5 23.0 fusion.42
  2212.6 397.2 %all-reduce.16.cloned.1.call-done = (f32[1,1024,1024]{1,2,0:T(8,128)}, f32[1,1024,1024]{1,2,0:T(8,128)}, f32[1,1024,1024]{1,2,0:T(8,128)}, f32[1,1024,1024]{1,2,...) async-done(((f32[1,1024,1024]{1,2,0:T(8,128)}, f32[1,1024,1024]{1,2,0:T(8,128)}, ...) | async-done | bytes 33554448 | tf_op jit(solution)/shard_map/psum | solution.py:38
  2609.7 12.0 pad_maximum_fusion
  2621.7 16.4 copy.9
  2638.1 12.0 pad_maximum_fusion.1
  (51 shorter events, 0.2 us)
Async XLA Ops:
  7.2 1534.8 %all-reduce.10.cloned.1.call-start = ((), (), s32[]{:S(2)}) async-start(), calls=%async_computation | async-start | bytes 16777216 | tf_op jit(solution)/shard_map/psum | solution.py:41
  14.6 2.0 copy-start.11
  317.5 7.9 copy-start
  325.4 1.9 copy-start.12
  621.6 7.9 copy-start.2
  629.5 2.0 copy-start.15
  924.5 7.9 copy-start.4
  932.4 1.9 copy-start.18
  1220.7 8.0 copy-start.19
  1228.7 12.0 copy-start.5
  1240.8 1.9 copy-start.21
  1251.1 607.5 %all-reduce.12.cloned.1.call-start = ((), (), s32[]{:S(2)}) async-start(), calls=%async_computation.1 | async-start | bytes 16777216 | tf_op jit(solution)/shard_map/psum | solution.py:41
  1542.0 6.4 copy-start.16
  1548.3 12.0 copy-start.7
  1560.4 2.0 copy-start.22
  1570.7 604.6 %all-reduce.14.cloned.1.call-start = ((), (), s32[]{:S(2)}) async-start(), calls=%async_computation.2 | async-start | bytes 16777216 | tf_op jit(solution)/shard_map/psum | solution.py:41
  1858.6 6.4 copy-start.13
  1865.0 12.0 copy-start.9
  1877.0 2.0 copy-start.24
  1887.4 722.3 %all-reduce.16.cloned.1.call-start = ((), (), s32[]{:S(2)}) async-start(), calls=%async_computation.3 | async-start | bytes 67108864 | tf_op jit(solution)/shard_map/psum | solution.py:38
  1887.5 10.2 copy-start.6
  1887.5 10.2 copy-start.20
  1897.7 6.6 copy-start.3
  1897.7 6.6 copy-start.23
  1904.3 6.2 copy-start.8
  1904.3 6.2 copy-start.17
  1910.5 6.5 copy-start.1
  1910.5 6.5 copy-start.25
  1917.0 6.2 copy-start.10
  1917.0 6.2 copy-start.14
Sparse Core Ops, SparseCore 0:
  1251.2 290.6 all-reduce.9
  1570.9 287.6 all-reduce.11
  1887.5 287.7 all-reduce.13
  2212.7 397.0 all-reduce.15
where the time goes:
time: 2660 us
  waiting for transfers between devices  1220 us (46%)
  blocking collectives  1120 us (42%)
  matrix products  208 us (8%)
  other arithmetic  61.3 us (2%)
  local copies, waits for them, and re-layouts  30.2 us (1%)
    psum x4, blocking collectives, local_step(): branch = lax.psum(part_out, 'tp').astype(jnp.bfloat16)  1120 us
    psum x3, waiting for transfers between devices, local_step(): lax.psum(back_part, 'tp')  823 us
    psum x1, waiting for transfers between devices, local_step(): grads_up[layer] = lax.psum(g_up, 'dp')  397 us
  transfers between devices with their start and end apart: 4, of which 4 were waited for; matrix products, arithmetic and copies ran while one was open for 2% of the time, Pallas kernels for 0%

commit v1 on v0

v1 whole, which is shorter than its diff:
```python
import functools
import math
import jax
import jax.numpy as jnp
from jax import lax
from jax.experimental import pallas as pl
from jax.experimental.pallas import tpu as pltpu
from jax.sharding import PartitionSpec as P

BF16 = jnp.bfloat16
F32 = jnp.float32
MESH = pl.DeviceIdType.MESH
TILES = 4
K0 = math.sqrt(2.0 / math.pi)
K1 = 0.044715 * K0
BY_ROWS = (((0,), (0,)), ((), ()))
BY_COLS = (((1,), (1,)), ((), ()))


def dot_cols(lhs, rhs):
    return lax.dot_general(lhs, rhs, BY_COLS, preferred_element_type=F32)


def dot_rows(lhs, rhs):
    return lax.dot_general(lhs, rhs, BY_ROWS, preferred_element_type=F32)


class Place:
    def __init__(self):
        z = lax.axis_index("tp")
        d = lax.axis_index("dp")
        self.core = lax.rem(d, 2)
        self.x = lax.rem(lax.div(d, 2), 2)
        self.y = lax.div(d, 4)
        self.across = {
            1: {"tp": z + 1 - 2 * lax.rem(z, 2)},
            2: {"tp": lax.rem(z + 2, 4)},
            3: {"tp": 3 - z},
        }
        self.x_dev = {"dp": self.index(self.y, 1 - self.x, self.core)}
        self.y_dev = {"dp": self.index(1 - self.y, self.x, self.core)}
        self.partner = {"dp": self.index(self.y, self.x, 1 - self.core)}

    @staticmethod
    def index(y, x, core):
        return y * 4 + x * 2 + core


def remote(src, dst, send_sem, recv_sem, device):
    return pltpu.make_async_remote_copy(src_ref=src, dst_ref=dst, send_sem=send_sem, recv_sem=recv_sem, device_id=device, device_id_type=MESH)


def meet(devices):
    barrier = pltpu.get_barrier_semaphore()
    for device in devices:
        pl.semaphore_signal(barrier, inc=1, device_id=device, device_id_type=MESH)
    pl.semaphore_wait(barrier, len(devices))


def forward_kernel(
    layers, total, x_ref, t_ref, up_ref, down_ref, w_ref, u_ref, a_ref, h_ref, g_ref,
    h_v, y_v, t_v, w_v, u_v, a_v, w_sem, u_sem, a_sem, h_sem, t_sem,
    zs, zr, xs, xr, ys, yr, as_, ar, bs, br, ds, dr,
):
    me = Place()
    groups = 3 * layers
    m, d = h_v.shape
    tm = m // TILES
    part = d // 8
    half = part // 2
    meet([me.across[1], me.across[2], me.across[3], me.x_dev, me.y_dev, me.partner])

    def rows(y, x):
        return pl.multiple_of(me.core * (4 * part) + (y * 2 + x) * part, part)

    mine, of_x, of_y, of_d = rows(me.y, me.x), rows(me.y, 1 - me.x), rows(1 - me.y, me.x), rows(1 - me.y, 1 - me.x)
    half_mine = pl.multiple_of(me.core * (4 * part), 4 * part)
    half_other = pl.multiple_of((1 - me.core) * (4 * part), 4 * part)

    def piece(c, start, size):
        return w_ref.at[c, :, pl.ds(start, size), :]

    def z_copy(c, s):
        return remote(piece(c, mine, part), piece(c, mine, part), zs.at[c], zr.at[c], me.across[s])

    def x_copy(c, start):
        return remote(piece(c, start, part), piece(c, start, part), xs.at[c], xr.at[c], me.x_dev)

    def y_copy(c, start):
        return remote(piece(c, start, part), piece(c, start, part), ys.at[c], yr.at[c], me.y_dev)

    def a_copy(c, start):
        return remote(piece(c, start, half), piece(c, start, half), as_.at[c], ar.at[c], me.y_dev)

    def b_copy(c, start):
        return remote(piece(c, start + half, half), piece(c, start + half, half), bs.at[c], br.at[c], me.x_dev)

    def d_copy(c, start):
        return remote(piece(c, start, 4 * part), piece(c, start, 4 * part), ds.at[c], dr.at[c], me.partner)

    def fetch_layer(l):
        for s in (1, 2, 3):
            c = 3 * l + s - 1
            for k, own in enumerate((up_ref, down_ref)):
                remote(own.at[l, pl.ds(mine, part), :], w_ref.at[c, k, pl.ds(mine, part), :], zs.at[c], zr.at[c], me.across[s]).start()

    def stage1(c):
        z_copy(c, 1).wait_recv()
        x_copy(c, mine).start()
        y_copy(c, mine).start()

    def stage2(c):
        x_copy(c, of_x).wait_recv()
        a_copy(c, of_x).start()
        y_copy(c, of_y).wait_recv()
        b_copy(c, of_y).start()

    def stage3(c):
        a_copy(c, of_d).wait_recv()
        b_copy(c, of_d).wait_recv()
        d_copy(c, half_mine).start()

    fetch_layer(0)
    fetch_layer(1)
    first = pltpu.make_async_copy(x_ref, h_v, t_sem.at[0])
    first.start()
    last = pltpu.make_async_copy(t_ref, t_v, t_sem.at[1])
    last.start()
    y_v[...] = jnp.zeros_like(y_v)
    first.wait()
    last.wait()

    def u_copy(it, t, slot):
        return pltpu.make_async_copy(u_v.at[slot], u_ref.at[it, pl.ds(t * tm, tm), :], u_sem.at[slot])

    def a_out(l, t, slot):
        return pltpu.make_async_copy(a_v.at[slot], a_ref.at[l, pl.ds(t * tm, tm), :], a_sem.at[slot])

    def h_out(dst, t):
        return pltpu.make_async_copy(h_v.at[pl.ds(t * tm, tm), :], dst.at[pl.ds(t * tm, tm), :], h_sem.at[t])

    def group(it, carry):
        l, s = lax.div(it, 4), lax.rem(it, 4)
        c = 3 * l + s - 1

        @pl.when((s == 0) & (l + 2 < layers))
        def _():
            fetch_layer(l + 2)

        @pl.when((s > 0) & (c + 1 < groups))
        def _():
            stage2(c + 1)

        @pl.when(s == 0)
        def _():
            pltpu.make_async_copy(up_ref.at[l], w_v.at[0], w_sem.at[0]).start()
            pltpu.make_async_copy(down_ref.at[l], w_v.at[1], w_sem.at[1]).start()

        @pl.when(s > 0)
        def _():
            d_copy(c, half_other).wait_recv()
            pltpu.make_async_copy(w_ref.at[c, 0], w_v.at[0], w_sem.at[0]).start()
            pltpu.make_async_copy(w_ref.at[c, 1], w_v.at[1], w_sem.at[1]).start()

        for k in (0, 1):
            pltpu.make_async_copy(up_ref.at[l], w_v.at[k], w_sem.at[k]).wait()

        def tile(t, carry):
            n = it * TILES + t
            slot = lax.rem(t, 2)
            here = pl.ds(pl.multiple_of(t * tm, tm), tm)

            @pl.when(n >= 2)
            def _():
                u_copy(it, t, slot).wait()

            @pl.when((n >= 2) & (lax.rem(lax.div(n - 2, TILES), 4) == 0))
            def _():
                a_out(l, t, slot).wait()

            wide = min(256, d)
            for j in range(0, d, wide):
                u = jnp.dot(h_v[here, :], w_v[0, :, j:j + wide], preferred_element_type=F32).astype(BF16)
                u_v[slot, :, j:j + wide] = u
                v = u.astype(F32)
                th = jnp.tanh(v * (K0 + K1 * (v * v)))
                hv = 0.5 * v
                a_v[slot, :, j:j + wide] = (hv + hv * th).astype(BF16)
            u_copy(it, t, slot).start()

            @pl.when(s == 0)
            def _():
                a_out(l, t, slot).start()

            for j in range(0, d, wide):
                y_v[here, j:j + wide] += jnp.dot(a_v[slot], w_v[1, :, j:j + wide], preferred_element_type=F32)

            @pl.when(s == 3)
            def _():
                @pl.when(l > 0)
                def _():
                    h_out(g_ref, t).wait()

                h_new = (h_v[here, :].astype(F32) + y_v[here, :].astype(BF16).astype(F32)).astype(BF16)
                y_v[here, :] = jnp.zeros((tm, d), F32)

                @pl.when(l < layers - 1)
                def _():
                    h_v[here, :] = h_new
                    h_out(h_ref.at[l], t).start()

                @pl.when(l == layers - 1)
                def _():
                    h_v[here, :] = ((h_new.astype(F32) - t_v[here, :].astype(F32)) / total).astype(BF16)
                    h_out(g_ref, t).start()

            @pl.when((it == 0) & (t == 0))
            def _():
                stage1(0)

            @pl.when((it == 0) & (t == 1))
            def _():
                stage1(1)
                stage2(0)

            @pl.when((it == 0) & (t == 3))
            def _():
                stage3(0)

            @pl.when((s > 0) & (t == 0) & (c + 2 < groups))
            def _():
                stage1(c + 2)

            @pl.when((s > 0) & (t == 2) & (c + 1 < groups))
            def _():
                stage3(c + 1)

            return carry

        lax.fori_loop(0, TILES, tile, 0)
        return carry

    lax.fori_loop(0, 4 * layers, group, 0)
    for slot in (0, 1):
        u_copy(0, slot, slot).wait()
    for t in range(TILES):
        h_out(g_ref, t).wait()

    def drain(c, carry):
        z_copy(c, 1).wait_send()
        x_copy(c, mine).wait_send()
        y_copy(c, mine).wait_send()
        a_copy(c, of_x).wait_send()
        b_copy(c, of_y).wait_send()
        d_copy(c, half_mine).wait_send()
        return carry

    lax.fori_loop(0, groups, drain, 0)


def backward_kernel(
    layers, x_ref, h_ref, up_ref, down_ref, w_ref, u_ref, a_ref, g_ref, gu_ref, gd_ref,
    g_v, acc_v, w_v, u_v, d_v, a_v, h_v, sums, in1, in2, in3, w_sem, u_sem, a_sem, h_sem, g_sem, out_sem, free1,
    s1, r1, s2, r2, s3, r3, s4, r4, s5, r5, s6, r6,
):
    me = Place()
    m, d = g_v.shape
    tm = m // TILES
    hd, qd = d // 2, d // 4
    e8, e16 = d // 8, d // 16
    wide = min(256, d)
    chunks = d // wide
    meet([me.x_dev, me.y_dev, me.partner])

    def at(value, size):
        return pl.ds(pl.multiple_of(value, size), size)

    own = me.core * hd
    own_rows, other_rows = at(own, hd), at(hd - own, hd)
    a_base, b_base = own, own + qd
    a_keep, a_give = at(a_base + me.x * e8, e8), at(a_base + (1 - me.x) * e8, e8)
    b_keep, b_give = at(b_base + me.y * e8, e8), at(b_base + (1 - me.y) * e8, e8)
    a_last, a_pass = at(a_base + me.x * e8 + me.y * e16, e16), at(a_base + me.x * e8 + (1 - me.y) * e16, e16)
    b_last, b_pass = at(b_base + me.y * e8 + me.x * e16, e16), at(b_base + me.y * e8 + (1 - me.x) * e16, e16)

    def c1(j):
        return remote(sums.at[lax.rem(j, 4), other_rows, :], in1.at[lax.rem(j, 2)], s1.at[j], r1.at[j], me.partner)

    def c2(j):
        q, r = lax.rem(j, 4), lax.rem(j, 2)
        return (remote(sums.at[q, a_give, :], in2.at[r, 0], s2.at[0, j], r2.at[0, j], me.x_dev),
                remote(sums.at[q, b_give, :], in2.at[r, 1], s2.at[1, j], r2.at[1, j], me.y_dev))

    def c3(j):
        q, r = lax.rem(j, 4), lax.rem(j, 2)
        return (remote(sums.at[q, a_pass, :], in3.at[r, 0], s3.at[0, j], r3.at[0, j], me.y_dev),
                remote(sums.at[q, b_pass, :], in3.at[r, 1], s3.at[1, j], r3.at[1, j], me.x_dev))

    def c4(j, ref, a_rows, b_rows):
        q, dst = lax.rem(j, 4), ref.at[layers - 1 - lax.div(j, 2)]
        return (remote(sums.at[q, a_rows, :], dst.at[a_rows, :], s4.at[0, j], r4.at[0, j], me.y_dev),
                remote(sums.at[q, b_rows, :], dst.at[b_rows, :], s4.at[1, j], r4.at[1, j], me.x_dev))

    def keep(j, ref):
        q, dst = lax.rem(j, 4), ref.at[layers - 1 - lax.div(j, 2)]
        return (pltpu.make_async_copy(sums.at[q, a_last, :], dst.at[a_last, :], out_sem.at[0, lax.rem(j, 2)]),
                pltpu.make_async_copy(sums.at[q, b_last, :], dst.at[b_last, :], out_sem.at[1, lax.rem(j, 2)]))

    def c5(j, ref, a_rows, b_rows):
        dst = ref.at[layers - 1 - lax.div(j, 2)]
        return (remote(dst.at[a_rows, :], dst.at[a_rows, :], s5.at[0, j], r5.at[0, j], me.x_dev),
                remote(dst.at[b_rows, :], dst.at[b_rows, :], s5.at[1, j], r5.at[1, j], me.y_dev))

    def c6(j, ref, which):
        dst = ref.at[layers - 1 - lax.div(j, 2)]
        return remote(dst.at[which, :], dst.at[which, :], s6.at[j], r6.at[j], me.partner)

    def add(j, start, size, buffer):
        q = lax.rem(j, 4)
        step = min(32, size)

        def body(i, carry):
            there = pl.ds(pl.multiple_of(start + i * step, step), step)
            sums[q, there, :] = sums[q, there, :] + buffer[pl.ds(pl.multiple_of(i * step, step), step), :]
            return carry

        lax.fori_loop(0, size // step, body, 0)

    def step1(j):
        @pl.when(j >= 2)
        def _():
            pl.semaphore_wait(free1, 1)

        c1(j).start()

    def step2(j):
        c1(j).wait_recv()
        add(j, own, hd, in1.at[lax.rem(j, 2)])

        @pl.when(j < 2 * layers - 2)
        def _():
            pl.semaphore_signal(free1, inc=1, device_id=me.partner, device_id_type=MESH)

        for copy in c2(j):
            copy.start()

    def step3(j):
        r, got, put = lax.rem(j, 2), c2(j), c3(j)
        for k, start in enumerate((a_base + me.x * e8, b_base + me.y * e8)):
            got[k].wait_recv()
            add(j, start, e8, in2.at[r, k])
            put[k].start()

    def step4(j, ref):
        r, got, put, local = lax.rem(j, 2), c3(j), c4(j, ref, a_last, b_last), keep(j, ref)
        for k, start in enumerate((a_base + me.x * e8 + me.y * e16, b_base + me.y * e8 + me.x * e16)):
            got[k].wait_recv()
            add(j, start, e16, in3.at[r, k])
            put[k].start()
            local[k].start()

    def step5(j, ref):
        got, put, local = c4(j, ref, a_pass, b_pass), c5(j, ref, a_keep, b_keep), keep(j, ref)
        for k in (0, 1):
            local[k].wait()
            got[k].wait_recv()
            put[k].start()

    def step6(j, ref):
        for copy in c5(j, ref, a_give, b_give):
            copy.wait_recv()
        c6(j, ref, own_rows).start()

    def step7(j, ref):
        c6(j, ref, other_rows).wait_recv()

    def settle(j, ref):
        c1(j).wait_send()
        for copy in c2(j) + c3(j) + c4(j, ref, a_last, b_last):
            copy.wait_send()

    def finish(j, ref):
        for copy in c5(j, ref, a_keep, b_keep):
            copy.wait_send()
        c6(j, ref, own_rows).wait_send()

    def u_copy(n):
        l, s, t = layers - 1 - lax.div(n, 16), lax.rem(lax.div(n, 4), 4), lax.rem(n, 4)
        slot = lax.rem(n, 2)
        return pltpu.make_async_copy(u_ref.at[4 * l + s, pl.ds(t * tm, tm), :], u_v.at[slot], u_sem.at[slot])

    def load_h(l):
        @pl.when(l == 0)
        def _():
            pltpu.make_async_copy(x_ref, h_v, h_sem).start()

        @pl.when(l > 0)
        def _():
            pltpu.make_async_copy(h_ref.at[l - 1], h_v, h_sem).start()

    def load_a(l):
        return pltpu.make_async_copy(a_ref.at[l], a_v, a_sem)

    def load_w(l, s):
        @pl.when(s == 0)
        def _():
            pltpu.make_async_copy(up_ref.at[l], w_v.at[0], w_sem.at[0]).start()
            pltpu.make_async_copy(down_ref.at[l], w_v.at[1], w_sem.at[1]).start()

        @pl.when(s > 0)
        def _():
            c = 3 * l + s - 1
            pltpu.make_async_copy(w_ref.at[c, 0], w_v.at[0], w_sem.at[0]).start()
            pltpu.make_async_copy(w_ref.at[c, 1], w_v.at[1], w_sem.at[1]).start()

    tiles_total = 16 * (layers - 1) + 4
    start_g = pltpu.make_async_copy(g_ref, g_v, g_sem)
    start_g.start()
    load_a(layers - 1).start()
    load_h(layers - 1)
    u_copy(0).start()
    start_g.wait()

    def layer(tau, carry):
        l = layers - 1 - tau
        down, up = 2 * tau, 2 * tau + 1
        qd_, qu_ = lax.rem(down, 4), lax.rem(up, 4)
        later = tau > 0
        load_w(l, 0)
        load_a(l).wait()

        @pl.when(tau >= 2)
        def _():
            settle(down - 4, gd_ref)

        def down_chunk(i, carry):
            k = lax.rem(i + (1 - me.core) * (chunks // 2), chunks)
            cols = pl.ds(pl.multiple_of(k * wide, wide), wide)
            sums[qd_, cols, :] = dot_rows(a_v[:, cols], g_v[...])

            @pl.when(i == chunks // 2 - 1)
            def _():
                step1(down)

                @pl.when(later)
                def _():
                    step5(down - 2, gd_ref)

            return carry

        lax.fori_loop(0, chunks, down_chunk, 0)

        @pl.when(l > 0)
        def _():
            load_a(l - 1).start()

        def block(s, carry):
            @pl.when(s > 0)
            def _():
                load_w(l, s)

            for k in (0, 1):
                pltpu.make_async_copy(up_ref.at[l], w_v.at[k], w_sem.at[k]).wait()

            def tile(t, carry):
                n = 16 * tau + 4 * s + t
                slot = lax.rem(n, 2)
                here = pl.ds(pl.multiple_of(t * tm, tm), tm)

                @pl.when(n + 1 < tiles_total)
                def _():
                    u_copy(n + 1).start()

                u_copy(n).wait()
                for j in range(0, d, wide):
                    da = dot_cols(g_v[here, :], w_v[1, j:j + wide, :])
                    v = u_v[slot, :, j:j + wide].astype(F32)
                    v2 = v * v
                    th = jnp.tanh(v * (K0 + K1 * v2))
                    slope = (0.5 + 0.5 * th) + (0.5 * v) * (1.0 - th * th) * (K0 + (3.0 * K1) * v2)
                    d_v[here, j:j + wide] = (da * slope).astype(BF16)

                @pl.when((l > 0) & (s == 0))
                def _():
                    for j in range(0, d, wide):
                        acc_v[here, j:j + wide] = g_v[here, j:j + wide].astype(F32) + dot_cols(d_v[here, :], w_v[0, j:j + wide, :])

                @pl.when((s > 0) & (s < 3))
                def _():
                    for j in range(0, d, wide):
                        acc_v[here, j:j + wide] += dot_cols(d_v[here, :], w_v[0, j:j + wide, :])

                @pl.when(s == 3)
                def _():
                    for j in range(0, d, wide):
                        total = acc_v[here, j:j + wide] + dot_cols(d_v[here, :], w_v[0, j:j + wide, :])
                        g_v[here, j:j + wide] = total.astype(BF16)

                def when(cond, run):
                    @pl.when(cond)
                    def _():
                        run()

                when((s == 0) & (t == 0), lambda: step2(down))
                when((s == 0) & (t == 1) & later, lambda: step4(down - 1, gu_ref))
                when((s == 0) & (t == 2) & later, lambda: step6(down - 2, gd_ref))
                when((s == 1) & (t == 1) & later, lambda: step5(down - 1, gu_ref))
                when((s == 1) & (t == 3), lambda: step2(up))
                when((s == 2) & (t == 0), lambda: step4(down, gd_ref))
                when((s == 2) & (t == 1) & later, lambda: step6(down - 1, gu_ref))
                when((s == 3) & (t == 0) & later, lambda: step7(down - 1, gu_ref))
                when((s == 3) & (t == 3), lambda: step3(up))
                return carry

            lax.fori_loop(0, TILES, tile, 0)

            @pl.when(s == 0)
            def _():
                pltpu.make_async_copy(x_ref, h_v, h_sem).wait()

                @pl.when(tau >= 2)
                def _():
                    settle(up - 4, gu_ref)

                def up_chunk(i, carry):
                    k = lax.rem(i + (1 - me.core) * (chunks // 2), chunks)
                    cols = pl.ds(pl.multiple_of(k * wide, wide), wide)
                    sums[qu_, cols, :] = dot_rows(h_v[:, cols], d_v[...])

                    @pl.when(i == chunks // 2 - 1)
                    def _():
                        step1(up)

                    return carry

                lax.fori_loop(0, chunks, up_chunk, 0)

                @pl.when(l > 0)
                def _():
                    load_h(l - 1)

                @pl.when(later)
                def _():
                    step7(down - 2, gd_ref)

                step3(down)

            return carry

        lax.fori_loop(0, jnp.where(l > 0, 4, 1), block, 0)
        return carry

    lax.fori_loop(0, layers, layer, 0)
    down, up = 2 * layers - 2, 2 * layers - 1
    step5(down - 1, gu_ref)
    step2(up)
    step4(down, gd_ref)
    step6(down - 1, gu_ref)
    step3(up)
    step7(down - 1, gu_ref)
    step5(down, gd_ref)
    step4(up, gu_ref)
    step6(down, gd_ref)
    step5(up, gu_ref)
    step7(down, gd_ref)
    step6(up, gu_ref)
    step7(up, gu_ref)

    def drain(tau, carry):
        finish(2 * tau, gd_ref)
        finish(2 * tau + 1, gu_ref)

        @pl.when(tau >= layers - 2)
        def _():
            settle(2 * tau, gd_ref)
            settle(2 * tau + 1, gu_ref)

        return carry

    lax.fori_loop(0, layers, drain, 0)


def any_specs(count):
    return [pl.BlockSpec(memory_space=pl.ANY)] * count


def local_step(hidden, targets, w_up, w_down, total_tokens):
    layers, d, own = w_up.shape
    m = hidden.shape[0]
    tm = m // TILES
    groups = 3 * layers
    dma = pltpu.SemaphoreType.DMA
    weights, acts, acts_own, states, g_last = pl.pallas_call(
        functools.partial(forward_kernel, layers, float(total_tokens)),
        out_shape=[
            jax.ShapeDtypeStruct((groups, 2, d, own), BF16),
            jax.ShapeDtypeStruct((4 * layers, m, own), BF16),
            jax.ShapeDtypeStruct((layers, m, own), BF16),
            jax.ShapeDtypeStruct((layers - 1, m, d), BF16),
            jax.ShapeDtypeStruct((m, d), BF16),
        ],
        in_specs=any_specs(4),
        out_specs=any_specs(5),
        scratch_shapes=[
            pltpu.VMEM((m, d), BF16),
            pltpu.VMEM((m, d), F32),
            pltpu.VMEM((m, d), BF16),
            pltpu.VMEM((2, d, own), BF16),
            pltpu.VMEM((2, tm, own), BF16),
            pltpu.VMEM((2, tm, own), BF16),
            dma((2,)), dma((2,)), dma((2,)), dma((TILES,)), dma((2,)),
        ] + [dma((groups,))] * 12,
        compiler_params=pltpu.CompilerParams(collective_id=0, has_side_effects=True, vmem_limit_bytes=60 << 20),
        name="forward",
    )(hidden, targets, w_up, w_down)
    grad_up, grad_down = pl.pallas_call(
        functools.partial(backward_kernel, layers),
        out_shape=[jax.ShapeDtypeStruct((layers, d, own), F32), jax.ShapeDtypeStruct((layers, own, d), F32)],
        in_specs=any_specs(8),
        out_specs=any_specs(2),
        scratch_shapes=[
            pltpu.VMEM((m, d), BF16),
            pltpu.VMEM((m, d), F32),
            pltpu.VMEM((2, d, own), BF16),
            pltpu.VMEM((2, tm, own), BF16),
            pltpu.VMEM((m, own), BF16),
            pltpu.VMEM((m, own), BF16),
            pltpu.VMEM((m, d), BF16),
            pltpu.VMEM((4, d, own), F32),
            pltpu.VMEM((2, d // 2, own), F32),
            pltpu.VMEM((2, 2, d // 8, own), F32),
            pltpu.VMEM((2, 2, d // 16, own), F32),
            dma((2,)), dma((2,)), dma, dma, dma, dma((2, 2)), pltpu.SemaphoreType.REGULAR,
            dma((2 * layers,)), dma((2 * layers,)),
        ] + [dma((2, 2 * layers))] * 8 + [dma((2 * layers,)), dma((2 * layers,))],
        compiler_params=pltpu.CompilerParams(collective_id=1, has_side_effects=True, vmem_limit_bytes=63 << 20),
        name="backward",
    )(hidden, states, w_up, w_down, weights, acts, acts_own, g_last)
    return grad_up, grad_down


def solution(mesh):
    def grad_step(hidden_in, targets, w_up, w_down):
        step_fn = functools.partial(local_step, total_tokens=hidden_in.shape[0])
        mapped = jax.shard_map(step_fn, mesh=mesh, in_specs=(P("dp", None), P("dp", None), P(None, None, "tp"), P(None, "tp", None)), out_specs=(P(None, None, "tp"), P(None, "tp", None)), check_vma=False)
        return mapped(hidden_in, targets, w_up, w_down)

    return grad_step
```

time: 2660 us -> 688 us (0.26)
  waiting for transfers between devices: 1220 us -> 0 us
  blocking collectives: 1120 us -> 0 us
  Pallas kernels: 0 us -> 665 us
  matrix products: 208 us -> 0 us
  other arithmetic: 61.3 us -> 0 us
    psum x4 -> x0, waiting for transfers between devices: 1220 us -> none  [the longest x3 823 us: local_step(): lax.psum(back_part, 'tp')]
    psum x4 -> x0, blocking collectives: 1120 us -> none  [local_step(): branch = lax.psum(part_out, 'tp').astype(jnp.bfloat16)]
    pallas_call x0 -> x2, Pallas kernels: none -> 665 us  [the longest x1 347 us: local_step(): pl.pallas_call(functools.partial(backward_kernel, layers), out_shape=[jax...]
    dot_general x22 -> x0, matrix products: 208 us -> none  [the longest x4 45.6 us: local_step(): lax.dot_general(h_in, d_pre, ROW_CONTRACT, preferred_element_type=jnp.flo...]
  transfers between devices with their start and end apart: 4 -> 0, of which waited for: 4 -> 0; matrix products, arithmetic and copies ran while one was open for 2% -> 0% of each run, Pallas kernels for 0% -> 0%
where the time goes in v1:
time: 688 us
  Pallas kernels  665 us (97%)
  local copies, waits for them, and re-layouts  22.6 us (3%)
    pallas_call x1, Pallas kernels, local_step(): pl.pallas_call(functools.partial(backward_kernel, layers), out_shape=[jax...  347 us
    pallas_call x1, Pallas kernels, local_step(): pl.pallas_call(functools.partial(forward_kernel, layers, float(total_toke...  317 us
    unnamed x4, local copies, waits for them, and re-layouts  22.6 us

profile of v1, /device:TPU:0, one launch (start us, length us, event | category | flops | bytes accessed | tf_op | source)
XLA Modules:
  0.0 688.1 jit_solution(9963412621189968592)
XLA Ops:
  0.6 317.4 %forward.1 = (bf16[12,2,1024,1024]{3,2,1,0:T(8,128)(2,1)}, bf16[16,2048,1024]{2,1,0:T(8,128)(2,1)}, bf16[4,2048,1024]{2,1,0:T(8,128)(2,1)}, bf16[3,2048,1024]{2,1,0:T(8,128)(2,1)}, bf16[2048,1024]{1,0:T(8,128)(2,1)}) custom-call(bf16[2048,1024]{1,0:T(8,128)(2,1)} %x_ref.3, bf16[2048,1024]{1,0:T(8,128)(2,1)} %t_ref.1, bf16[4,1024,1024]{2,1,0:T(8,128)(2,1)} %up_ref.3, ...), custom_call_target="tpu_custom_call" | custom-call | tf_op jit(solution)/shard_map/forward/pallas_call | solution.py:593
  318.0 347.4 %backward.1 = (f32[4,1024,1024]{2,1,0:T(8,128)}, f32[4,1024,1024]{2,1,0:T(8,128)}) custom-call(bf16[2048,1024]{1,0:T(8,128)(2,1)} %x_ref.3, bf16[3,2048,1024]{2,1,0:T(8,128)(2,1)} %get-tuple-element.7.h_ref, bf16[4,1024,1024]{2,1,0:T(8,128)(2,1)} %up_ref.3, bf16[4,1024,1024]{2,1,0:T(8,128)(2,1)} %down_ref.3, ...), custom_call_target="tpu_custom_call" | custom-call | tf_op jit(solution)/shard_map/backward/pallas_call | solution.py:616
  665.5 0.0 copy-start
  665.5 12.8 %copy.8 = f32[4,1024,1024]{2,1,0:T(8,128)} copy(f32[4,1024,1024]{2,1,0:T(8,128)} %get-tuple-element.14) | data formatting | bytes 33554432
  678.3 3.6 copy-done
  681.9 6.2 copy.9
Async XLA Ops:
  665.5 16.4 %copy-start = (f32[4,1024,1024]{2,1,0:T(8,128)S(1)}, f32[4,1024,1024]{2,1,0:T(8,128)}, u32[]{:S(2)}) copy-start(f32[4,1024,1024]{2,1,0:T(8,128)} %get-tuple-element.15) | copy-start | bytes 50331652

commit v2 on v0

v2 whole, which is shorter than its diff:
```python
import functools
import math
import jax
import jax.numpy as jnp
from jax import lax
from jax.experimental import pallas as pl
from jax.experimental.pallas import tpu as pltpu
from jax.sharding import PartitionSpec as P

BF16 = jnp.bfloat16
F32 = jnp.float32
MESH = pl.DeviceIdType.MESH
TILES = 4
K0 = math.sqrt(2.0 / math.pi)
K1 = 0.044715 * K0
BY_ROWS = (((0,), (0,)), ((), ()))
BY_COLS = (((1,), (1,)), ((), ()))


def dot_cols(lhs, rhs):
    return lax.dot_general(lhs, rhs, BY_COLS, preferred_element_type=F32)


def dot_rows(lhs, rhs):
    return lax.dot_general(lhs, rhs, BY_ROWS, preferred_element_type=F32)


class Place:
    def __init__(self):
        z = lax.axis_index("tp")
        d = lax.axis_index("dp")
        self.core = lax.rem(d, 2)
        self.x = lax.rem(lax.div(d, 2), 2)
        self.y = lax.div(d, 4)
        self.inner = (z == 1) | (z == 2)
        self.near = {"tp": z + 1 - 2 * lax.rem(z, 2)}
        self.middle = {"tp": 3 - z}
        self.x_dev = {"dp": self.index(self.y, 1 - self.x, self.core)}
        self.y_dev = {"dp": self.index(1 - self.y, self.x, self.core)}
        self.partner = {"dp": self.index(self.y, self.x, 1 - self.core)}

    @staticmethod
    def index(y, x, core):
        return y * 4 + x * 2 + core


def remote(src, dst, send_sem, recv_sem, device):
    return pltpu.make_async_remote_copy(src_ref=src, dst_ref=dst, send_sem=send_sem, recv_sem=recv_sem, device_id=device, device_id_type=MESH)


def meet(devices):
    barrier = pltpu.get_barrier_semaphore()
    for device in devices:
        pl.semaphore_signal(barrier, inc=1, device_id=device, device_id_type=MESH)
    pl.semaphore_wait(barrier, len(devices))


FORWARD_TIMES = {
    "F": (0, 0, 1, 3, 3, 6, 18, 16, 25, 29, 31, 36),
    "Z": (2, 5, 22),
    "1": (0, 0, 2, 5, 7, 12, 20, 20, 29, 33, 36, 44),
    "2": (2, 3, 4, 11, 14, 19, 25, 29, 35, 42, 45, 53),
    "3": (3, 6, 7, 15, 20, 24, 31, 33, 40, 47, 52, 56),
    "L": (3, 7, 10, 12, 18, 23, 26, 30, 33, 37, 42, 45, 49, 54, 58),
}

BACKWARD_TIMES = (
    (0, 6, 32, 38, 64, 70, 96, 102),
    (2, 8, 34, 40, 66, 72, 98, 128),
    (6, 12, 41, 44, 73, 76, 130, 131),
    (9, 16, 46, 47, 78, 79, 132, 133),
    (14, 32, 49, 51, 81, 83, 134, 135),
    (19, 37, 66, 69, 98, 103, 136, 138),
    (32, 39, 68, 71, 101, 129, 137, 139),
)


def forward_plan():
    events = []
    for rank, (kind, times) in enumerate(FORWARD_TIMES.items()):
        for i, n in enumerate(times):
            c = i + 1 if kind in "ZL" else i
            age = 3 * c - 2.5 if kind == "Z" else c if kind != "L" else 3 * (c // 4) + (c % 4 - 1 if c % 4 else -0.5)
            events.append((n, age, rank, kind, c))
    return [(n, kind, c) for n, _, _, kind, c in sorted(events)]


def backward_plan():
    return [(p, k, j) for p, j, k in sorted((p, j, k + 1) for k, times in enumerate(BACKWARD_TIMES) for j, p in enumerate(times))]


def at_step(plan, now, block, steps, run):
    for b in sorted({e[0] // block for e in plan}):
        here = [e for e in plan if e[0] // block == b and e[0] % block in steps]
        if not here:
            continue

        @pl.when(lax.div(now, block) == b)
        def _():
            for n in sorted({e[0] for e in here}):
                @pl.when(now == n)
                def _():
                    for e in here:
                        if e[0] == n:
                            run(e[1], e[2])


def forward_pass(
    layers, total, prefetch, x_ref, t_ref, up_ref, down_ref, w_ref, u_ref, a_ref, h_ref,
    h_v, y_v, t_v, w_v, u_v, a_v, w_sem, u_sem, a_sem, h_sem, t_sem,
    zs, zr, fs, xs, xr, ys, yr, as_, ar, bs, br, ds, dr,
):
    plan = forward_plan()
    me = Place()
    groups = 3 * layers
    m, d = h_v.shape
    tm = m // TILES
    part = d // 8
    half = part // 2
    last_n = 4 * TILES * layers - 1
    wide = min(256, d)

    def rows(y, x):
        return pl.multiple_of(me.core * (4 * part) + (y * 2 + x) * part, part)

    mine, of_x, of_y, of_d = rows(me.y, me.x), rows(me.y, 1 - me.x), rows(1 - me.y, me.x), rows(1 - me.y, 1 - me.x)
    half_mine = pl.multiple_of(me.core * (4 * part), 4 * part)
    half_other = pl.multiple_of((1 - me.core) * (4 * part), 4 * part)

    def piece(c, start, size):
        return w_ref.at[c, :, pl.ds(start, size), :]

    def z_copy(c):
        return remote(piece(c, mine, part), piece(c, mine, part), zs.at[c], zr.at[c], me.near)

    def f_copy(c):
        to, device = (c + 2, me.middle) if c % 3 == 0 else (c, me.near)
        return remote(piece(c, mine, part), piece(to, mine, part), fs.at[c], zr.at[to], device)

    def x_copy(c, start):
        return remote(piece(c, start, part), piece(c, start, part), xs.at[c], xr.at[c], me.x_dev)

    def y_copy(c, start):
        return remote(piece(c, start, part), piece(c, start, part), ys.at[c], yr.at[c], me.y_dev)

    def a_copy(c, start):
        return remote(piece(c, start, half), piece(c, start, half), as_.at[c], ar.at[c], me.y_dev)

    def b_copy(c, start):
        return remote(piece(c, start + half, half), piece(c, start + half, half), bs.at[c], br.at[c], me.x_dev)

    def d_copy(c, start):
        return remote(piece(c, start, 4 * part), piece(c, start, 4 * part), ds.at[c], dr.at[c], me.partner)

    def send_own(l, c, device):
        for k, own in enumerate((up_ref, down_ref)):
            remote(own.at[l, pl.ds(mine, part), :], w_ref.at[c, k, pl.ds(mine, part), :], zs.at[c], zr.at[c], device).start()

    def load_w(g):
        l, s, ws = g // 4, g % 4, g % 2
        c = 3 * l + s - 1
        if s > 0:
            d_copy(c, half_other).wait_recv()
        for k, own in enumerate((up_ref, down_ref)):
            pltpu.make_async_copy(own.at[l] if s == 0 else w_ref.at[c, k], w_v.at[ws, k], w_sem.at[ws, k]).start()

    def run(kind, c):
        if kind == "Z":
            send_own(c, 3 * c, me.near)

            @pl.when(me.inner)
            def _():
                send_own(c, 3 * c + 1, me.middle)
        elif kind == "F":
            @pl.when(me.inner)
            def _():
                z_copy(c).wait_recv()
                f_copy(c).start()
        elif kind == "1":
            @pl.when(jnp.logical_not(me.inner))
            def _():
                z_copy(c).wait_recv()

            x_copy(c, mine).start()
            y_copy(c, mine).start()
        elif kind == "2":
            x_copy(c, of_x).wait_recv()
            a_copy(c, of_x).start()
            y_copy(c, of_y).wait_recv()
            b_copy(c, of_y).start()
        elif kind == "3":
            a_copy(c, of_d).wait_recv()
            b_copy(c, of_d).wait_recv()
            d_copy(c, half_mine).start()
        else:
            load_w(c)

    first = pltpu.make_async_copy(x_ref, h_v, t_sem.at[0])
    first.start()
    load_w(0)
    meet([me.near, me.middle, me.x_dev, me.y_dev, me.partner])
    run("Z", 0)
    last = pltpu.make_async_copy(t_ref, t_v, t_sem.at[1])
    last.start()
    y_v[...] = jnp.zeros_like(y_v)
    first.wait()

    def tile_of(n):
        return lax.rem(n, TILES)

    def there(n):
        return pl.ds(pl.multiple_of(tile_of(n) * tm, tm), tm)

    def slot_of(n):
        return lax.rem(lax.div(n, TILES), 2)

    def wait_w(n):
        for k in (0, 1):
            pltpu.make_async_copy(up_ref.at[0], w_v.at[slot_of(n), k], w_sem.at[slot_of(n), k]).wait()

    def u_copy(n):
        slot = lax.rem(n, 2)
        return pltpu.make_async_copy(u_v.at[slot], u_ref.at[lax.div(n, TILES), there(n), :], u_sem.at[slot])

    def a_out(n):
        slot = lax.rem(n, 2)
        return pltpu.make_async_copy(a_v.at[slot], a_ref.at[lax.div(n, 4 * TILES), there(n), :], a_sem.at[slot])

    def h_out(dst, n):
        return pltpu.make_async_copy(h_v.at[there(n), :], dst.at[there(n), :], h_sem.at[tile_of(n)])

    def is_block(n, s):
        return lax.rem(lax.div(n, TILES), 4) == s

    def settle_rows(n):
        l = lax.div(n, 4 * TILES)

        @pl.when(l > 0)
        def _():
            h_out(h_ref.at[0], n).wait()

        def sweep(last_layer):
            size = min(32, tm)

            def body(i, carry):
                few = pl.ds(pl.multiple_of(tile_of(n) * tm + i * size, size), size)
                h_new = (h_v[few, :].astype(F32) + y_v[few, :].astype(BF16).astype(F32)).astype(BF16)
                if last_layer:
                    h_new = ((h_new.astype(F32) - t_v[few, :].astype(F32)) / total).astype(BF16)
                h_v[few, :] = h_new
                y_v[few, :] = h_new.astype(F32) if last_layer else jnp.zeros((size, d), F32)
                return carry

            lax.fori_loop(0, tm // size, body, 0)

        @pl.when(l < layers - 1)
        def _():
            sweep(False)
            h_out(h_ref.at[l], n).start()

        @pl.when(l == layers - 1)
        def _():
            sweep(True)

    def step(n, carry):
        here, slot, ws = there(n), lax.rem(n, 2), slot_of(n)

        @pl.when(n >= 2)
        def _():
            u_copy(n).wait()

        @pl.when((n >= 2) & is_block(n - 2, 0))
        def _():
            a_out(n).wait()

        @pl.when(tile_of(n) == 0)
        def _():
            wait_w(n)

        for j in range(0, d, wide):
            u = jnp.dot(h_v[here, :], w_v[ws, 0, :, j:j + wide], preferred_element_type=F32).astype(BF16)
            u_v[slot, :, j:j + wide] = u
            v = u.astype(F32)
            th = jnp.tanh(v * (K0 + K1 * (v * v)))
            hv = 0.5 * v
            a_v[slot, :, j:j + wide] = (hv + hv * th).astype(BF16)
        u_copy(n).start()

        @pl.when(is_block(n, 0))
        def _():
            a_out(n).start()

        @pl.when(n == last_n - TILES + 1)
        def _():
            prefetch()

        at_step(plan, n, 4 * TILES, range(4 * TILES), run)
        for j in range(0, d, wide):
            y_v[here, j:j + wide] += jnp.dot(a_v[slot], w_v[ws, 1, :, j:j + wide], preferred_element_type=F32)

        @pl.when(is_block(n, 3))
        def _():
            settle_rows(n)

        return carry

    last.wait()
    lax.fori_loop(0, last_n + 1, step, 0)
    u_copy(last_n - 1).wait()
    u_copy(last_n).wait()

    def drain():
        for c in range(groups):
            if c % 3 == 0:
                z_copy(c).wait_send()

            @pl.when(me.inner)
            def _():
                f_copy(c).wait_send()
                if c % 3 == 1:
                    z_copy(c).wait_send()

            x_copy(c, mine).wait_send()
            y_copy(c, mine).wait_send()
            a_copy(c, of_x).wait_send()
            b_copy(c, of_y).wait_send()
            d_copy(c, half_mine).wait_send()

    return drain


def backward_pass(
    layers, load_a, load_w, x_ref, h_ref, up_ref, u_ref, gu_ref, gd_ref,
    g_v, acc_v, w_v, u_v, d_v, a_v, h_v, sums, in1, in2, in3,
    w_sem, u_sem, h_sem, out_sem, free1,
    s1, r1, s2, r2, s3, r3, s4, r4, s5, r5, s6, r6,
):
    plan = backward_plan()
    me = Place()
    m, d = g_v.shape
    tm = m // TILES
    hd, qd = d // 2, d // 4
    e8, e16 = d // 8, d // 16
    wide = min(256, d)
    broad = d // 2

    def at(value, size):
        return pl.ds(pl.multiple_of(value, size), size)

    own = me.core * hd
    own_rows, other_rows = at(own, hd), at(hd - own, hd)
    a_base, b_base = own, own + qd
    a_keep, a_give = at(a_base + me.x * e8, e8), at(a_base + (1 - me.x) * e8, e8)
    b_keep, b_give = at(b_base + me.y * e8, e8), at(b_base + (1 - me.y) * e8, e8)
    a_last, a_pass = at(a_base + me.x * e8 + me.y * e16, e16), at(a_base + me.x * e8 + (1 - me.y) * e16, e16)
    b_last, b_pass = at(b_base + me.y * e8 + me.x * e16, e16), at(b_base + me.y * e8 + (1 - me.x) * e16, e16)

    def room(j):
        return lax.rem(j, 2) * (1 + lax.rem(lax.div(j, 2), 2))

    def c1(j):
        return remote(sums.at[room(j), other_rows, :], in1.at[lax.rem(j, 2)], s1.at[j], r1.at[j], me.partner)

    def c2(j):
        q, r = room(j), lax.rem(j, 2)
        return (remote(sums.at[q, a_give, :], in2.at[r, 0], s2.at[0, j], r2.at[0, j], me.x_dev),
                remote(sums.at[q, b_give, :], in2.at[r, 1], s2.at[1, j], r2.at[1, j], me.y_dev))

    def c3(j):
        q, r = room(j), lax.rem(j, 2)
        return (remote(sums.at[q, a_pass, :], in3.at[r, 0], s3.at[0, j], r3.at[0, j], me.y_dev),
                remote(sums.at[q, b_pass, :], in3.at[r, 1], s3.at[1, j], r3.at[1, j], me.x_dev))

    def c4(j, ref, a_rows, b_rows):
        q, dst = room(j), ref.at[layers - 1 - lax.div(j, 2)]
        return (remote(sums.at[q, a_rows, :], dst.at[a_rows, :], s4.at[0, j], r4.at[0, j], me.y_dev),
                remote(sums.at[q, b_rows, :], dst.at[b_rows, :], s4.at[1, j], r4.at[1, j], me.x_dev))

    def keep(j, ref):
        q, dst = room(j), ref.at[layers - 1 - lax.div(j, 2)]
        return (pltpu.make_async_copy(sums.at[q, a_last, :], dst.at[a_last, :], out_sem.at[0, lax.rem(j, 2)]),
                pltpu.make_async_copy(sums.at[q, b_last, :], dst.at[b_last, :], out_sem.at[1, lax.rem(j, 2)]))

    def c5(j, ref, a_rows, b_rows):
        dst = ref.at[layers - 1 - lax.div(j, 2)]
        return (remote(dst.at[a_rows, :], dst.at[a_rows, :], s5.at[0, j], r5.at[0, j], me.x_dev),
                remote(dst.at[b_rows, :], dst.at[b_rows, :], s5.at[1, j], r5.at[1, j], me.y_dev))

    def c6(j, ref, which):
        dst = ref.at[layers - 1 - lax.div(j, 2)]
        return remote(dst.at[which, :], dst.at[which, :], s6.at[j], r6.at[j], me.partner)

    def add(j, start, size, buffer):
        q = room(j)
        step = min(32, size)

        def body(i, carry):
            there = pl.ds(pl.multiple_of(start + i * step, step), step)
            sums[q, there, :] = sums[q, there, :] + buffer[pl.ds(pl.multiple_of(i * step, step), step), :]
            return carry

        lax.fori_loop(0, size // step, body, 0)

    def step1(j):
        @pl.when(j >= 2)
        def _():
            pl.semaphore_wait(free1, 1)

        c1(j).start()

    def step2(j):
        c1(j).wait_recv()
        add(j, own, hd, in1.at[lax.rem(j, 2)])

        @pl.when(j < 2 * layers - 2)
        def _():
            pl.semaphore_signal(free1, inc=1, device_id=me.partner, device_id_type=MESH)

        for copy in c2(j):
            copy.start()

    def step3(j):
        r, got, put = lax.rem(j, 2), c2(j), c3(j)
        for k, start in enumerate((a_base + me.x * e8, b_base + me.y * e8)):
            got[k].wait_recv()
            add(j, start, e8, in2.at[r, k])
            put[k].start()

    def step4(j, ref):
        r, got, put, local = lax.rem(j, 2), c3(j), c4(j, ref, a_last, b_last), keep(j, ref)
        for k, start in enumerate((a_base + me.x * e8 + me.y * e16, b_base + me.y * e8 + me.x * e16)):
            got[k].wait_recv()
            add(j, start, e16, in3.at[r, k])
            put[k].start()
            local[k].start()

    def step5(j, ref):
        got, put, local = c4(j, ref, a_pass, b_pass), c5(j, ref, a_keep, b_keep), keep(j, ref)
        for k in (0, 1):
            local[k].wait()
            got[k].wait_recv()
            put[k].start()

    def step6(j, ref):
        for copy in c5(j, ref, a_give, b_give):
            copy.wait_recv()
        c6(j, ref, own_rows).start()

    def step7(j, ref):
        c6(j, ref, other_rows).wait_recv()

    def settle(j, ref):
        c1(j).wait_send()
        for copy in c2(j) + c3(j) + c4(j, ref, a_last, b_last):
            copy.wait_send()

    def finish(j, ref):
        for copy in c5(j, ref, a_keep, b_keep):
            copy.wait_send()
        c6(j, ref, own_rows).wait_send()

    def run(k, j):
        ref = gd_ref if j % 2 == 0 else gu_ref
        (step1, step2, step3, step4, step5, step6, step7)[k - 1](*((j,) if k <= 3 else (j, ref)))

    def at_place(tau, p, steps):
        at_step(plan, 32 * tau + p, 32, steps, run)

    def u_copy(n):
        l, s, t, slot = layers - 1 - lax.div(n, 16), lax.rem(lax.div(n, 4), 4), lax.rem(n, 4), lax.rem(n, 2)
        return pltpu.make_async_copy(u_ref.at[4 * l + s, pl.ds(t * tm, tm), :], u_v.at[slot], u_sem.at[slot])

    def load_h(l):
        @pl.when(l == 0)
        def _():
            pltpu.make_async_copy(x_ref, h_v, h_sem).start()

        @pl.when(l > 0)
        def _():
            pltpu.make_async_copy(h_ref.at[l - 1], h_v, h_sem).start()

    def wait_w(i):
        for k in (0, 1):
            pltpu.make_async_copy(up_ref.at[0], w_v.at[lax.rem(i, 2), k], w_sem.at[lax.rem(i, 2), k]).wait()

    def next_g():
        step = min(64, m)

        def body(i, carry):
            here = pl.ds(pl.multiple_of(i * step, step), step)
            g_v[here, :] = acc_v[here, :].astype(BF16)
            acc_v[here, :] = g_v[here, :].astype(F32)
            return carry

        lax.fori_loop(0, m // step, body, 0)

    load_h(layers - 1)
    u_copy(0).start()
    tiles_total = 16 * (layers - 1) + 4
    groups = 4 * (layers - 1) + 1

    def layer(tau, carry):
        l = layers - 1 - tau
        down, up = 2 * tau, 2 * tau + 1
        room_down, room_up = room(down), room(up)
        load_a(l).wait()

        @pl.when(tau > 0)
        def _():
            settle(down - 2, gd_ref)

        def product(room_j, lhs, rhs, base):
            def body(i, carry):
                cols = at(lax.rem(i + 1 + me.core, 2) * broad, broad)
                sums[room_j, cols, :] = dot_rows(lhs[:, cols], rhs[...])
                at_place(tau, base + i, (base, base + 1))
                return carry

            lax.fori_loop(0, 2, body, 0)

        product(room_down, a_v, g_v, 0)

        @pl.when(l > 0)
        def _():
            load_a(l - 1).start()

        def step(n, carry):
            k = 16 * tau + n
            block, slot = 4 * tau + lax.div(n, TILES), lax.rem(k, 2)
            ws = lax.rem(block, 2)
            here = pl.ds(pl.multiple_of(lax.rem(n, TILES) * tm, tm), tm)

            @pl.when(k + 1 < tiles_total)
            def _():
                u_copy(k + 1).start()

            @pl.when(lax.rem(n, TILES) == 0)
            def _():
                @pl.when(block + 1 < groups)
                def _():
                    load_w(block + 1)

                wait_w(block)

            u_copy(k).wait()
            for j in range(0, d, wide):
                da = dot_cols(g_v[here, :], w_v[ws, 1, j:j + wide, :])
                v = u_v[slot, :, j:j + wide].astype(F32)
                v2 = v * v
                th = jnp.tanh(v * (K0 + K1 * v2))
                slope = (1.0 + th) * (0.5 + (v * (1.0 - th)) * ((0.5 * K0) + (1.5 * K1) * v2))
                d_v[here, j:j + wide] = (da * slope).astype(BF16)
            at_place(tau, n + jnp.where(n >= 4, 4, 2), list(range(2, 6)) + list(range(8, 20)))

            @pl.when(l > 0)
            def _():
                for j in range(0, d, wide):
                    acc_v[here, j:j + wide] += dot_cols(d_v[here, :], w_v[ws, 0, j:j + wide, :])

            @pl.when(n == TILES - 1)
            def _():
                pltpu.make_async_copy(x_ref, h_v, h_sem).wait()

                @pl.when(tau >= 2)
                def _():
                    settle(up - 4, gu_ref)

                product(room_up, h_v, d_v, 6)

                @pl.when(l > 0)
                def _():
                    load_h(l - 1)

            return carry

        lax.fori_loop(0, jnp.where(l > 0, 16, 4), step, 0)

        @pl.when(l > 0)
        def _():
            next_g()
            at_place(tau, 20, (20,))

        return carry

    lax.fori_loop(0, layers, layer, 0)
    for p, k, j in plan:
        if p >= 32 * layers:
            run(k, j)
    for j in range(2 * layers):
        ref = gd_ref if j % 2 == 0 else gu_ref
        finish(j, ref)
        if j >= 2 * layers - 3 and j != 2 * layers - 4:
            settle(j, ref)


def kernel(
    layers, total, x_ref, t_ref, up_ref, down_ref, w_ref, u_ref, a_ref, h_ref, gu_ref, gd_ref,
    h_v, y_v, t_v, w_v, u_v, act_v, d_v, a_v, sums, in1, in2, in3,
    w_sem, u_sem, act_sem, h_sem, t_sem, back_u_sem, back_a_sem, back_h_sem, out_sem, free1, *sems,
):
    def load_a(l):
        return pltpu.make_async_copy(a_ref.at[l], a_v, back_a_sem)

    def load_w(i):
        l, s = layers - 1 - lax.div(i, 4), lax.rem(i, 4)
        ws = lax.rem(i, 2)

        @pl.when(s == 0)
        def _():
            pltpu.make_async_copy(up_ref.at[l], w_v.at[ws, 0], w_sem.at[ws, 0]).start()
            pltpu.make_async_copy(down_ref.at[l], w_v.at[ws, 1], w_sem.at[ws, 1]).start()

        @pl.when(s > 0)
        def _():
            c = 3 * l + s - 1
            for k in (0, 1):
                pltpu.make_async_copy(w_ref.at[c, k], w_v.at[ws, k], w_sem.at[ws, k]).start()

    def prefetch():
        load_a(layers - 1).start()
        load_w(0)

    drain = forward_pass(
        layers, total, prefetch, x_ref, t_ref, up_ref, down_ref, w_ref, u_ref, a_ref, h_ref,
        h_v, y_v, t_v, w_v, u_v, act_v, w_sem, u_sem, act_sem, h_sem, t_sem, *sems[:13],
    )
    backward_pass(
        layers, load_a, load_w, x_ref, h_ref, up_ref, u_ref, gu_ref, gd_ref,
        h_v, y_v, w_v, u_v, d_v, a_v, t_v, sums, in1, in2, in3,
        w_sem, back_u_sem, back_h_sem, out_sem, free1, *sems[13:],
    )
    drain()


def any_specs(count):
    return [pl.BlockSpec(memory_space=pl.ANY)] * count


def local_step(hidden, targets, w_up, w_down, total_tokens):
    layers, d, own = w_up.shape
    m = hidden.shape[0]
    tm = m // TILES
    groups = 3 * layers
    dma = pltpu.SemaphoreType.DMA
    out = pl.pallas_call(
        functools.partial(kernel, layers, float(total_tokens)),
        out_shape=[
            jax.ShapeDtypeStruct((groups, 2, d, own), BF16),
            jax.ShapeDtypeStruct((4 * layers, m, own), BF16),
            jax.ShapeDtypeStruct((layers, m, own), BF16),
            jax.ShapeDtypeStruct((layers - 1, m, d), BF16),
            jax.ShapeDtypeStruct((layers, d, own), F32),
            jax.ShapeDtypeStruct((layers, own, d), F32),
        ],
        in_specs=any_specs(4),
        out_specs=any_specs(6),
        scratch_shapes=[
            pltpu.VMEM((m, d), BF16),
            pltpu.VMEM((m, d), F32),
            pltpu.VMEM((m, d), BF16),
            pltpu.VMEM((2, 2, d, own), BF16),
            pltpu.VMEM((2, tm, own), BF16),
            pltpu.VMEM((2, tm, own), BF16),
            pltpu.VMEM((m, own), BF16),
            pltpu.VMEM((m, own), BF16),
            pltpu.VMEM((3, d, own), F32),
            pltpu.VMEM((2, d // 2, own), F32),
            pltpu.VMEM((2, 2, d // 8, own), F32),
            pltpu.VMEM((2, 2, d // 16, own), F32),
            dma((2, 2)), dma((2,)), dma((2,)), dma((TILES,)), dma((2,)),
            dma((2,)), dma, dma, dma((2, 2)), pltpu.SemaphoreType.REGULAR,
        ] + [dma((groups,))] * 13 + [dma((2 * layers,))] * 2 + [dma((2, 2 * layers))] * 8 + [dma((2 * layers,))] * 2,
        compiler_params=pltpu.CompilerParams(collective_id=0, has_side_effects=True, vmem_limit_bytes=66_900_000),
        name="gradients",
    )(hidden, targets, w_up, w_down)
    return out[4], out[5]


def solution(mesh):
    def grad_step(hidden_in, targets, w_up, w_down):
        step_fn = functools.partial(local_step, total_tokens=hidden_in.shape[0])
        mapped = jax.shard_map(step_fn, mesh=mesh, in_specs=(P("dp", None), P("dp", None), P(None, None, "tp"), P(None, "tp", None)), out_specs=(P(None, None, "tp"), P(None, "tp", None)), check_vma=False)
        return mapped(hidden_in, targets, w_up, w_down)

    return grad_step
```

time: 2660 us -> 578 us (0.22)
  waiting for transfers between devices: 1220 us -> 0 us
  blocking collectives: 1120 us -> 0 us
  Pallas kernels: 0 us -> 554 us
  matrix products: 208 us -> 0 us
  other arithmetic: 61.3 us -> 0 us
    psum x4 -> x0, waiting for transfers between devices: 1220 us -> none  [the longest x3 823 us: local_step(): lax.psum(back_part, 'tp')]
    psum x4 -> x0, blocking collectives: 1120 us -> none  [local_step(): branch = lax.psum(part_out, 'tp').astype(jnp.bfloat16)]
    pallas_call x0 -> x1, Pallas kernels: none -> 554 us  [local_step(): pl.pallas_call(functools.partial(kernel, layers, float(total_tokens)), ou...]
    dot_general x22 -> x0, matrix products: 208 us -> none  [the longest x4 45.6 us: local_step(): lax.dot_general(h_in, d_pre, ROW_CONTRACT, preferred_element_type=jnp.flo...]
  transfers between devices with their start and end apart: 4 -> 0, of which waited for: 4 -> 0; matrix products, arithmetic and copies ran while one was open for 2% -> 0% of each run, Pallas kernels for 0% -> 0%
where the time goes in v2:
time: 578 us
  Pallas kernels  554 us (96%)
  local copies, waits for them, and re-layouts  22.6 us (4%)
    pallas_call x1, Pallas kernels, local_step(): pl.pallas_call(functools.partial(kernel, layers, float(total_tokens)), ou...  554 us
    unnamed x4, local copies, waits for them, and re-layouts  22.6 us

profile of v2, /device:TPU:0, one launch (start us, length us, event | category | flops | bytes accessed | tf_op | source)
XLA Modules:
  0.0 577.7 jit_solution(10479988249920390821)
XLA Ops:
  0.6 554.5 %gradients.1 = (bf16[12,2,1024,1024]{3,2,1,0:T(8,128)(2,1)}, bf16[16,2048,1024]{2,1,0:T(8,128)(2,1)}, bf16[4,2048,1024]{2,1,0:T(8,128)(2,1)}, bf16[3,2048,1024]{...) custom-call(bf16[2048,1024]{1,0:T(8,128)(2,1)} %x_ref.1, bf16[2048,1024]{1,0:T(8,128)(2,1)} %t_ref.1, ...), custom_call_target="tpu_custom_call" | custom-call | tf_op jit(solution)/shard_map/gradients/pallas_call | solution.py:645
  555.1 0.0 copy-start
  555.1 12.8 %copy.8 = f32[4,1024,1024]{2,1,0:T(8,128)} copy(f32[4,1024,1024]{2,1,0:T(8,128)} %get-tuple-element.8) | data formatting | bytes 33554432
  567.9 3.6 copy-done
  571.5 6.2 %copy.9 = f32[4,1024,1024]{2,1,0:T(8,128)} copy(f32[4,1024,1024]{2,1,0:T(8,128)S(1)} %copy-done) | data formatting | bytes 33554432
Async XLA Ops:
  555.1 16.4 %copy-start = (f32[4,1024,1024]{2,1,0:T(8,128)S(1)}, f32[4,1024,1024]{2,1,0:T(8,128)}, u32[]{:S(2)}) copy-start(f32[4,1024,1024]{2,1,0:T(8,128)} %get-tuple-element.9) | copy-start | bytes 50331652

commit v3 on v2

--- a/solution.py
+++ b/solution.py
@@ -10,7 +10,9 @@
 BF16 = jnp.bfloat16
 F32 = jnp.float32
 MESH = pl.DeviceIdType.MESH
-TILES = 4
+TILES = 2
+PARTS_FORWARD = 8
+PARTS_BACKWARD = 4
 K0 = math.sqrt(2.0 / math.pi)
 K1 = 0.044715 * K0
 BY_ROWS = (((0,), (0,)), ((), ()))
@@ -56,22 +58,22 @@
 
 
 FORWARD_TIMES = {
-    "F": (0, 0, 1, 3, 3, 6, 18, 16, 25, 29, 31, 36),
-    "Z": (2, 5, 22),
-    "1": (0, 0, 2, 5, 7, 12, 20, 20, 29, 33, 36, 44),
-    "2": (2, 3, 4, 11, 14, 19, 25, 29, 35, 42, 45, 53),
-    "3": (3, 6, 7, 15, 20, 24, 31, 33, 40, 47, 52, 56),
-    "L": (3, 7, 10, 12, 18, 23, 26, 30, 33, 37, 42, 45, 49, 54, 58),
+    "F": (0, 0, 0, 1, 1, 5, 14, 16, 22, 11, 12, 23),
+    "Z": (1, 6, 1),
+    "1": (0, 0, 1, 3, 6, 13, 18, 21, 27, 36, 41, 47),
+    "2": (1, 1, 4, 7, 16, 18, 25, 32, 34, 44, 46, 54),
+    "3": (3, 5, 9, 14, 19, 24, 32, 36, 39, 48, 51, 57),
+    "L": (3, 6, 10, 12, 19, 23, 26, 29, 34, 38, 42, 46, 50, 54, 59),
 }
 
 BACKWARD_TIMES = (
     (0, 6, 32, 38, 64, 70, 96, 102),
-    (2, 8, 34, 40, 66, 72, 98, 128),
-    (6, 12, 41, 44, 73, 76, 130, 131),
-    (9, 16, 46, 47, 78, 79, 132, 133),
-    (14, 32, 49, 51, 81, 83, 134, 135),
-    (19, 37, 66, 69, 98, 103, 136, 138),
-    (32, 39, 68, 71, 101, 129, 137, 139),
+    (2, 8, 33, 40, 65, 71, 97, 128),
+    (7, 14, 39, 46, 74, 76, 133, 134),
+    (10, 19, 45, 51, 77, 79, 135, 137),
+    (15, 35, 48, 66, 81, 84, 143, 144),
+    (50, 42, 81, 80, 131, 131, 147, 151),
+    (99, 96, 145, 151, 145, 145, 151, 151),
 )
 
 
@@ -277,13 +279,16 @@
         def _():
             wait_w(n)
 
-        for j in range(0, d, wide):
-            u = jnp.dot(h_v[here, :], w_v[ws, 0, :, j:j + wide], preferred_element_type=F32).astype(BF16)
-            u_v[slot, :, j:j + wide] = u
-            v = u.astype(F32)
-            th = jnp.tanh(v * (K0 + K1 * (v * v)))
-            hv = 0.5 * v
-            a_v[slot, :, j:j + wide] = (hv + hv * th).astype(BF16)
+        few = tm // PARTS_FORWARD
+        for r in range(0, tm, few):
+            some = pl.ds(pl.multiple_of(tile_of(n) * tm + r, few), few)
+            for j in range(0, d, wide):
+                u = jnp.dot(h_v[some, :], w_v[ws, 0, :, j:j + wide], preferred_element_type=F32).astype(BF16)
+                u_v[slot, r:r + few, j:j + wide] = u
+                v = u.astype(F32)
+                th = jnp.tanh(v * (K0 + K1 * (v * v)))
+                hv = 0.5 * v
+                a_v[slot, r:r + few, j:j + wide] = (hv + hv * th).astype(BF16)
         u_copy(n).start()
 
         @pl.when(is_block(n, 0))
@@ -294,13 +299,15 @@
         def _():
             prefetch()
 
-        at_step(plan, n, 4 * TILES, range(4 * TILES), run)
+        at_step(plan, 2 * n, 8 * TILES, range(0, 8 * TILES, 2), run)
         for j in range(0, d, wide):
             y_v[here, j:j + wide] += jnp.dot(a_v[slot], w_v[ws, 1, :, j:j + wide], preferred_element_type=F32)
 
         @pl.when(is_block(n, 3))
         def _():
             settle_rows(n)
+
+        at_step(plan, 2 * n + 1, 8 * TILES, range(1, 8 * TILES, 2), run)
 
         return carry
 
@@ -467,7 +474,7 @@
         at_step(plan, 32 * tau + p, 32, steps, run)
 
     def u_copy(n):
-        l, s, t, slot = layers - 1 - lax.div(n, 16), lax.rem(lax.div(n, 4), 4), lax.rem(n, 4), lax.rem(n, 2)
+        l, s, t, slot = layers - 1 - lax.div(n, 4 * TILES), lax.rem(lax.div(n, TILES), 4), lax.rem(n, TILES), lax.rem(n, 2)
         return pltpu.make_async_copy(u_ref.at[4 * l + s, pl.ds(t * tm, tm), :], u_v.at[slot], u_sem.at[slot])
 
     def load_h(l):
@@ -496,7 +503,7 @@
 
     load_h(layers - 1)
     u_copy(0).start()
-    tiles_total = 16 * (layers - 1) + 4
+    tiles_total = TILES * (4 * (layers - 1) + 1)
     groups = 4 * (layers - 1) + 1
 
     def layer(tau, carry):
@@ -525,7 +532,7 @@
             load_a(l - 1).start()
 
         def step(n, carry):
-            k = 16 * tau + n
+            k = 4 * TILES * tau + n
             block, slot = 4 * tau + lax.div(n, TILES), lax.rem(k, 2)
             ws = lax.rem(block, 2)
             here = pl.ds(pl.multiple_of(lax.rem(n, TILES) * tm, tm), tm)
@@ -543,19 +550,25 @@
                 wait_w(block)
 
             u_copy(k).wait()
-            for j in range(0, d, wide):
-                da = dot_cols(g_v[here, :], w_v[ws, 1, j:j + wide, :])
-                v = u_v[slot, :, j:j + wide].astype(F32)
-                v2 = v * v
-                th = jnp.tanh(v * (K0 + K1 * v2))
-                slope = (1.0 + th) * (0.5 + (v * (1.0 - th)) * ((0.5 * K0) + (1.5 * K1) * v2))
-                d_v[here, j:j + wide] = (da * slope).astype(BF16)
-            at_place(tau, n + jnp.where(n >= 4, 4, 2), list(range(2, 6)) + list(range(8, 20)))
+            few = tm // PARTS_BACKWARD
+            for r in range(0, tm, few):
+                some = pl.ds(pl.multiple_of(lax.rem(n, TILES) * tm + r, few), few)
+                for j in range(0, d, wide):
+                    da = dot_cols(g_v[some, :], w_v[ws, 1, j:j + wide, :])
+                    v = u_v[slot, r:r + few, j:j + wide].astype(F32)
+                    v2 = v * v
+                    th = jnp.tanh(v * (K0 + K1 * v2))
+                    slope = (1.0 + th) * (0.5 + (v * (1.0 - th)) * ((0.5 * K0) + (1.5 * K1) * v2))
+                    d_v[some, j:j + wide] = (da * slope).astype(BF16)
+            place = 2 * n + jnp.where(n >= TILES, 4, 2)
+            at_place(tau, place, [2, 4] + list(range(8, 20, 2)))
 
             @pl.when(l > 0)
             def _():
                 for j in range(0, d, wide):
                     acc_v[here, j:j + wide] += dot_cols(d_v[here, :], w_v[ws, 0, j:j + wide, :])
+
+            at_place(tau, place + 1, [3, 5] + list(range(9, 20, 2)))
 
             @pl.when(n == TILES - 1)
             def _():
@@ -573,7 +586,7 @@
 
             return carry
 
-        lax.fori_loop(0, jnp.where(l > 0, 16, 4), step, 0)
+        lax.fori_loop(0, jnp.where(l > 0, 4 * TILES, TILES), step, 0)
 
         @pl.when(l > 0)
         def _():

time: 578 us -> 576 us (level)
  no operation moved by 1% of the time
where the time goes in v3:
time: 576 us; the launch traced here: 575 us
  Pallas kernels  552 us (96%)
  local copies, waits for them, and re-layouts  22.6 us (4%)
    pallas_call x1, Pallas kernels, local_step(): pl.pallas_call(functools.partial(kernel, layers, float(total_tokens)), ou...  552 us
    unnamed x4, local copies, waits for them, and re-layouts  22.6 us

profile of v3, /device:TPU:0, one launch (start us, length us, event | category | flops | bytes accessed | tf_op | source)
XLA Modules:
  0.0 575.5 jit_solution(2700662556979931115)
XLA Ops:
  0.6 552.2 %gradients.1 = (bf16[12,2,1024,1024]{3,2,1,0:T(8,128)(2,1)}, bf16[16,2048,1024]{2,1,0:T(8,128)(2,1)}, bf16[4,2048,1024]{2,1,0:T(8,128)(2,1)}, bf16[3,2048,1024]{...) custom-call(bf16[2048,1024]{1,0:T(8,128)(2,1)} %x_ref.1, bf16[2048,1024]{1,0:T(8,128)(2,1)} %t_ref.1, ...), custom_call_target="tpu_custom_call" | custom-call | tf_op jit(solution)/shard_map/gradients/pallas_call | solution.py:658
  552.9 0.0 copy-start
  552.9 12.8 %copy.8 = f32[4,1024,1024]{2,1,0:T(8,128)} copy(f32[4,1024,1024]{2,1,0:T(8,128)} %get-tuple-element.8) | data formatting | bytes 33554432
  565.7 3.6 copy-done
  569.3 6.2 %copy.9 = f32[4,1024,1024]{2,1,0:T(8,128)} copy(f32[4,1024,1024]{2,1,0:T(8,128)S(1)} %copy-done) | data formatting | bytes 33554432
Async XLA Ops:
  552.9 16.4 %copy-start = (f32[4,1024,1024]{2,1,0:T(8,128)S(1)}, f32[4,1024,1024]{2,1,0:T(8,128)}, u32[]{:S(2)}) copy-start(f32[4,1024,1024]{2,1,0:T(8,128)} %get-tuple-element.9) | copy-start | bytes 50331652

commit v4 on v3

--- a/solution.py
+++ b/solution.py
@@ -58,22 +58,22 @@
 
 
 FORWARD_TIMES = {
-    "F": (0, 0, 0, 1, 1, 5, 14, 16, 22, 11, 12, 23),
-    "Z": (1, 6, 1),
-    "1": (0, 0, 1, 3, 6, 13, 18, 21, 27, 36, 41, 47),
-    "2": (1, 1, 4, 7, 16, 18, 25, 32, 34, 44, 46, 54),
-    "3": (3, 5, 9, 14, 19, 24, 32, 36, 39, 48, 51, 57),
-    "L": (3, 6, 10, 12, 19, 23, 26, 29, 34, 38, 42, 46, 50, 54, 59),
+    "F": (0, 0, 0, 1, 2, 5, 14, 13, 24, 25, 25, 33),
+    "Z": (1, 6, 14),
+    "1": (0, 0, 1, 4, 7, 14, 20, 21, 30, 35, 38, 45),
+    "2": (1, 2, 4, 11, 17, 19, 28, 31, 35, 43, 48, 51),
+    "3": (2, 5, 7, 15, 20, 22, 32, 36, 38, 46, 51, 55),
+    "L": (3, 6, 9, 12, 17, 22, 25, 27, 34, 38, 42, 43, 49, 54, 58),
 }
 
 BACKWARD_TIMES = (
     (0, 6, 32, 38, 64, 70, 96, 102),
-    (2, 8, 33, 40, 65, 71, 97, 128),
-    (7, 14, 39, 46, 74, 76, 133, 134),
-    (10, 19, 45, 51, 77, 79, 135, 137),
-    (15, 35, 48, 66, 81, 84, 143, 144),
-    (50, 42, 81, 80, 131, 131, 147, 151),
-    (99, 96, 145, 151, 145, 145, 151, 151),
+    (2, 8, 34, 40, 66, 71, 98, 103),
+    (7, 13, 41, 44, 74, 75, 128, 128),
+    (11, 17, 46, 47, 77, 79, 131, 132),
+    (15, 33, 49, 51, 80, 82, 133, 134),
+    (83, 76, 148, 81, 103, 133, 137, 148),
+    (99, 103, 151, 135, 143, 138, 151, 149),
 )
 
 
@@ -110,7 +110,7 @@
 def forward_pass(
     layers, total, prefetch, x_ref, t_ref, up_ref, down_ref, w_ref, u_ref, a_ref, h_ref,
     h_v, y_v, t_v, w_v, u_v, a_v, w_sem, u_sem, a_sem, h_sem, t_sem,
-    zs, zr, fs, xs, xr, ys, yr, as_, ar, bs, br, ds, dr,
+    zs, zr, fs, ms, mr, mf, xs, xr, ys, yr, as_, ar, bs, br, ds, dr,
 ):
     plan = forward_plan()
     me = Place()
@@ -132,12 +132,18 @@
     def piece(c, start, size):
         return w_ref.at[c, :, pl.ds(start, size), :]
 
-    def z_copy(c):
-        return remote(piece(c, mine, part), piece(c, mine, part), zs.at[c], zr.at[c], me.near)
-
-    def f_copy(c):
+    def more(c):
+        return d // 64 if c >= 3 else 0
+
+    def z_rows(c):
+        return [(mine, part, zs, zr, fs)] + ([(of_d + half - more(c), 2 * more(c), ms, mr, mf)] if more(c) else [])
+
+    def z_copies(c):
+        return [remote(piece(c, start, size), piece(c, start, size), send.at[c], recv.at[c], me.near) for start, size, send, recv, _ in z_rows(c)]
+
+    def f_copies(c):
         to, device = (c + 2, me.middle) if c % 3 == 0 else (c, me.near)
-        return remote(piece(c, mine, part), piece(to, mine, part), fs.at[c], zr.at[to], device)
+        return [remote(piece(c, start, size), piece(to, start, size), send.at[c], recv.at[to], device) for start, size, _, recv, send in z_rows(c)]
 
     def x_copy(c, start):
         return remote(piece(c, start, part), piece(c, start, part), xs.at[c], xr.at[c], me.x_dev)
@@ -146,17 +152,21 @@
         return remote(piece(c, start, part), piece(c, start, part), ys.at[c], yr.at[c], me.y_dev)
 
     def a_copy(c, start):
-        return remote(piece(c, start, half), piece(c, start, half), as_.at[c], ar.at[c], me.y_dev)
+        size = half - more(c)
+        return remote(piece(c, start, size), piece(c, start, size), as_.at[c], ar.at[c], me.y_dev)
 
     def b_copy(c, start):
-        return remote(piece(c, start + half, half), piece(c, start + half, half), bs.at[c], br.at[c], me.x_dev)
+        start, size = start + half + more(c), half - more(c)
+        return remote(piece(c, start, size), piece(c, start, size), bs.at[c], br.at[c], me.x_dev)
 
     def d_copy(c, start):
         return remote(piece(c, start, 4 * part), piece(c, start, 4 * part), ds.at[c], dr.at[c], me.partner)
 
     def send_own(l, c, device):
-        for k, own in enumerate((up_ref, down_ref)):
-            remote(own.at[l, pl.ds(mine, part), :], w_ref.at[c, k, pl.ds(mine, part), :], zs.at[c], zr.at[c], device).start()
+        for start, size, send, recv, _ in z_rows(c):
+            for k, own in enumerate((up_ref, down_ref)):
+                there = w_ref.at[c, k, pl.ds(start, size), :]
+                remote(own.at[l, pl.ds(start, size), :], there, send.at[c], recv.at[c], device).start()
 
     def load_w(g):
         l, s, ws = g // 4, g % 4, g % 2
@@ -176,12 +186,15 @@
         elif kind == "F":
             @pl.when(me.inner)
             def _():
-                z_copy(c).wait_recv()
-                f_copy(c).start()
+                for copy in z_copies(c):
+                    copy.wait_recv()
+                for copy in f_copies(c):
+                    copy.start()
         elif kind == "1":
             @pl.when(jnp.logical_not(me.inner))
             def _():
-                z_copy(c).wait_recv()
+                for copy in z_copies(c):
+                    copy.wait_recv()
 
             x_copy(c, mine).start()
             y_copy(c, mine).start()
@@ -319,13 +332,13 @@
     def drain():
         for c in range(groups):
             if c % 3 == 0:
-                z_copy(c).wait_send()
+                for copy in z_copies(c):
+                    copy.wait_send()
 
             @pl.when(me.inner)
             def _():
-                f_copy(c).wait_send()
-                if c % 3 == 1:
-                    z_copy(c).wait_send()
+                for copy in f_copies(c) + (z_copies(c) if c % 3 == 1 else []):
+                    copy.wait_send()
 
             x_copy(c, mine).wait_send()
             y_copy(c, mine).wait_send()
@@ -635,12 +648,12 @@
 
     drain = forward_pass(
         layers, total, prefetch, x_ref, t_ref, up_ref, down_ref, w_ref, u_ref, a_ref, h_ref,
-        h_v, y_v, t_v, w_v, u_v, act_v, w_sem, u_sem, act_sem, h_sem, t_sem, *sems[:13],
+        h_v, y_v, t_v, w_v, u_v, act_v, w_sem, u_sem, act_sem, h_sem, t_sem, *sems[:16],
     )
     backward_pass(
         layers, load_a, load_w, x_ref, h_ref, up_ref, u_ref, gu_ref, gd_ref,
         h_v, y_v, w_v, u_v, d_v, a_v, t_v, sums, in1, in2, in3,
-        w_sem, back_u_sem, back_h_sem, out_sem, free1, *sems[13:],
+        w_sem, back_u_sem, back_h_sem, out_sem, free1, *sems[16:],
     )
     drain()
 
@@ -682,7 +695,7 @@
             pltpu.VMEM((2, 2, d // 16, own), F32),
             dma((2, 2)), dma((2,)), dma((2,)), dma((TILES,)), dma((2,)),
             dma((2,)), dma, dma, dma((2, 2)), pltpu.SemaphoreType.REGULAR,
-        ] + [dma((groups,))] * 13 + [dma((2 * layers,))] * 2 + [dma((2, 2 * layers))] * 8 + [dma((2 * layers,))] * 2,
+        ] + [dma((groups,))] * 16 + [dma((2 * layers,))] * 2 + [dma((2, 2 * layers))] * 8 + [dma((2 * layers,))] * 2,
         compiler_params=pltpu.CompilerParams(collective_id=0, has_side_effects=True, vmem_limit_bytes=66_900_000),
         name="gradients",
     )(hidden, targets, w_up, w_down)

time: 576 us -> 565 us (0.981)
  Pallas kernels: 552 us -> 541 us
    pallas_call x1, Pallas kernels: 552 us -> 541 us  [local_step(): pl.pallas_call(functools.partial(kernel, layers, float(total_tokens)), ou...]
where the time goes in v4:
time: 565 us; the launch traced here: 564 us
  Pallas kernels  541 us (96%)
  local copies, waits for them, and re-layouts  22.6 us (4%)
    pallas_call x1, Pallas kernels, local_step(): pl.pallas_call(functools.partial(kernel, layers, float(total_tokens)), ou...  541 us
    unnamed x4, local copies, waits for them, and re-layouts  22.6 us

profile of v4, /device:TPU:0, one launch (start us, length us, event | category | flops | bytes accessed | tf_op | source)
XLA Modules:
  0.0 564.5 jit_solution(455977598155045310)
XLA Ops:
  0.6 541.2 %gradients.1 = (bf16[12,2,1024,1024]{3,2,1,0:T(8,128)(2,1)}, bf16[16,2048,1024]{2,1,0:T(8,128)(2,1)}, bf16[4,2048,1024]{2,1,0:T(8,128)(2,1)}, bf16[3,2048,1024]{...) custom-call(bf16[2048,1024]{1,0:T(8,128)(2,1)} %x_ref.1, bf16[2048,1024]{1,0:T(8,128)(2,1)} %t_ref.1, ...), custom_call_target="tpu_custom_call" | custom-call | tf_op jit(solution)/shard_map/gradients/pallas_call | solution.py:671
  541.9 0.0 copy-start
  541.9 12.8 %copy.8 = f32[4,1024,1024]{2,1,0:T(8,128)} copy(f32[4,1024,1024]{2,1,0:T(8,128)} %get-tuple-element.8) | data formatting | bytes 33554432
  554.7 3.6 copy-done
  558.3 6.2 %copy.9 = f32[4,1024,1024]{2,1,0:T(8,128)} copy(f32[4,1024,1024]{2,1,0:T(8,128)S(1)} %copy-done) | data formatting | bytes 33554432
Async XLA Ops:
  541.9 16.4 %copy-start = (f32[4,1024,1024]{2,1,0:T(8,128)S(1)}, f32[4,1024,1024]{2,1,0:T(8,128)}, u32[]{:S(2)}) copy-start(f32[4,1024,1024]{2,1,0:T(8,128)} %get-tuple-element.9) | copy-start | bytes 50331652

commit v5 on v4

--- a/solution.py
+++ b/solution.py
@@ -58,12 +58,12 @@
 
 
 FORWARD_TIMES = {
-    "F": (0, 0, 0, 1, 2, 5, 14, 13, 24, 25, 25, 33),
-    "Z": (1, 6, 14),
-    "1": (0, 0, 1, 4, 7, 14, 20, 21, 30, 35, 38, 45),
-    "2": (1, 2, 4, 11, 17, 19, 28, 31, 35, 43, 48, 51),
-    "3": (2, 5, 7, 15, 20, 22, 32, 36, 38, 46, 51, 55),
-    "L": (3, 6, 9, 12, 17, 22, 25, 27, 34, 38, 42, 43, 49, 54, 58),
+    "F": (0, 0, 0, 3, 4, 7, 16, 14, 22, 24, 26, 31),
+    "Z": (2, 8, 17),
+    "1": (0, 0, 2, 7, 8, 14, 20, 23, 32, 38, 39, 49),
+    "2": (2, 4, 5, 13, 16, 20, 27, 30, 37, 46, 47, 54),
+    "3": (3, 6, 8, 16, 21, 23, 32, 33, 41, 49, 53, 57),
+    "L": (3, 7, 9, 14, 18, 22, 24, 29, 34, 35, 42, 45, 50, 54, 58),
 }
 
 BACKWARD_TIMES = (
@@ -122,12 +122,14 @@
     last_n = 4 * TILES * layers - 1
     wide = min(256, d)
 
-    def rows(y, x):
-        return pl.multiple_of(me.core * (4 * part) + (y * 2 + x) * part, part)
-
-    mine, of_x, of_y, of_d = rows(me.y, me.x), rows(me.y, 1 - me.x), rows(1 - me.y, me.x), rows(1 - me.y, 1 - me.x)
-    half_mine = pl.multiple_of(me.core * (4 * part), 4 * part)
-    half_other = pl.multiple_of((1 - me.core) * (4 * part), 4 * part)
+    def rows(y, x, core):
+        return pl.multiple_of(core * (4 * part) + (y * 2 + x) * part, part)
+
+    def square(core):
+        return [rows(y, x, core) for y, x in ((me.y, me.x), (me.y, 1 - me.x), (1 - me.y, me.x), (1 - me.y, 1 - me.x))]
+
+    ours, partners = square(me.core), square(1 - me.core)
+    mine, of_x, of_y, of_d = ours
 
     def piece(c, start, size):
         return w_ref.at[c, :, pl.ds(start, size), :]
@@ -159,8 +161,9 @@
         start, size = start + half + more(c), half - more(c)
         return remote(piece(c, start, size), piece(c, start, size), bs.at[c], br.at[c], me.x_dev)
 
-    def d_copy(c, start):
-        return remote(piece(c, start, 4 * part), piece(c, start, 4 * part), ds.at[c], dr.at[c], me.partner)
+    def d_copy(c, i, starts):
+        there = piece(c, starts[i], part)
+        return remote(there, there, ds.at[i, c], dr.at[i, c], me.partner)
 
     def send_own(l, c, device):
         for start, size, send, recv, _ in z_rows(c):
@@ -172,7 +175,8 @@
         l, s, ws = g // 4, g % 4, g % 2
         c = 3 * l + s - 1
         if s > 0:
-            d_copy(c, half_other).wait_recv()
+            for i in range(4):
+                d_copy(c, i, partners).wait_recv()
         for k, own in enumerate((up_ref, down_ref)):
             pltpu.make_async_copy(own.at[l] if s == 0 else w_ref.at[c, k], w_v.at[ws, k], w_sem.at[ws, k]).start()
 
@@ -198,15 +202,18 @@
 
             x_copy(c, mine).start()
             y_copy(c, mine).start()
+            d_copy(c, 0, ours).start()
         elif kind == "2":
             x_copy(c, of_x).wait_recv()
             a_copy(c, of_x).start()
             y_copy(c, of_y).wait_recv()
             b_copy(c, of_y).start()
+            d_copy(c, 1, ours).start()
+            d_copy(c, 2, ours).start()
         elif kind == "3":
             a_copy(c, of_d).wait_recv()
             b_copy(c, of_d).wait_recv()
-            d_copy(c, half_mine).start()
+            d_copy(c, 3, ours).start()
         else:
             load_w(c)
 
@@ -344,7 +351,8 @@
             y_copy(c, mine).wait_send()
             a_copy(c, of_x).wait_send()
             b_copy(c, of_y).wait_send()
-            d_copy(c, half_mine).wait_send()
+            for i in range(4):
+                d_copy(c, i, ours).wait_send()
 
     return drain
 
@@ -695,7 +703,7 @@
             pltpu.VMEM((2, 2, d // 16, own), F32),
             dma((2, 2)), dma((2,)), dma((2,)), dma((TILES,)), dma((2,)),
             dma((2,)), dma, dma, dma((2, 2)), pltpu.SemaphoreType.REGULAR,
-        ] + [dma((groups,))] * 16 + [dma((2 * layers,))] * 2 + [dma((2, 2 * layers))] * 8 + [dma((2 * layers,))] * 2,
+        ] + [dma((groups,))] * 14 + [dma((4, groups))] * 2 + [dma((2 * layers,))] * 2 + [dma((2, 2 * layers))] * 8 + [dma((2 * layers,))] * 2,
         compiler_params=pltpu.CompilerParams(collective_id=0, has_side_effects=True, vmem_limit_bytes=66_900_000),
         name="gradients",
     )(hidden, targets, w_up, w_down)

time: 565 us -> 566 us (level)
  no operation moved by 1% of the time
where the time goes in v5:
time: 566 us
  Pallas kernels  542 us (96%)
  local copies, waits for them, and re-layouts  22.6 us (4%)
    pallas_call x1, Pallas kernels, local_step(): pl.pallas_call(functools.partial(kernel, layers, float(total_tokens)), ou...  542 us
    unnamed x4, local copies, waits for them, and re-layouts  22.6 us

profile of v5, /device:TPU:0, one launch (start us, length us, event | category | flops | bytes accessed | tf_op | source)
XLA Modules:
  0.0 565.7 jit_solution(17965012697736575990)
XLA Ops:
  0.6 542.5 %gradients.1 = (bf16[12,2,1024,1024]{3,2,1,0:T(8,128)(2,1)}, bf16[16,2048,1024]{2,1,0:T(8,128)(2,1)}, bf16[4,2048,1024]{2,1,0:T(8,128)(2,1)}, bf16[3,2048,1024]{...) custom-call(bf16[2048,1024]{1,0:T(8,128)(2,1)} %x_ref.1, bf16[2048,1024]{1,0:T(8,128)(2,1)} %t_ref.1, ...), custom_call_target="tpu_custom_call" | custom-call | tf_op jit(solution)/shard_map/gradients/pallas_call | solution.py:679
  543.1 0.0 copy-start
  543.1 12.8 %copy.8 = f32[4,1024,1024]{2,1,0:T(8,128)} copy(f32[4,1024,1024]{2,1,0:T(8,128)} %get-tuple-element.8) | data formatting | bytes 33554432
  556.0 3.6 copy-done
  559.5 6.2 %copy.9 = f32[4,1024,1024]{2,1,0:T(8,128)} copy(f32[4,1024,1024]{2,1,0:T(8,128)S(1)} %copy-done) | data formatting | bytes 33554432
Async XLA Ops:
  543.1 16.4 %copy-start = (f32[4,1024,1024]{2,1,0:T(8,128)S(1)}, f32[4,1024,1024]{2,1,0:T(8,128)}, u32[]{:S(2)}) copy-start(f32[4,1024,1024]{2,1,0:T(8,128)} %get-tuple-element.9) | copy-start | bytes 50331652

commit v6 on v4

--- a/solution.py
+++ b/solution.py
@@ -58,12 +58,12 @@
 
 
 FORWARD_TIMES = {
-    "F": (0, 0, 0, 1, 2, 5, 14, 13, 24, 25, 25, 33),
-    "Z": (1, 6, 14),
-    "1": (0, 0, 1, 4, 7, 14, 20, 21, 30, 35, 38, 45),
-    "2": (1, 2, 4, 11, 17, 19, 28, 31, 35, 43, 48, 51),
-    "3": (2, 5, 7, 15, 20, 22, 32, 36, 38, 46, 51, 55),
-    "L": (3, 6, 9, 12, 17, 22, 25, 27, 34, 38, 42, 43, 49, 54, 58),
+    "F": (0, 0, 0, 3, 3, 6, 15, 16, 21, 30, 33, 36),
+    "Z": (1, 8, 22),
+    "1": (0, 0, 1, 5, 7, 12, 20, 23, 28, 35, 40, 44),
+    "2": (1, 2, 4, 12, 17, 19, 26, 33, 35, 43, 48, 51),
+    "3": (3, 5, 7, 15, 20, 22, 32, 36, 39, 47, 52, 54),
+    "L": (3, 6, 9, 11, 18, 22, 25, 27, 34, 38, 41, 46, 50, 54, 56),
 }
 
 BACKWARD_TIMES = (

time: 565 us -> 566 us (level)
  no operation moved by 1% of the time
where the time goes in v6:
time: 566 us
  Pallas kernels  543 us (96%)
  local copies, waits for them, and re-layouts  22.6 us (4%)
    pallas_call x1, Pallas kernels, local_step(): pl.pallas_call(functools.partial(kernel, layers, float(total_tokens)), ou...  543 us
    unnamed x4, local copies, waits for them, and re-layouts  22.6 us

profile of v6, /device:TPU:0, one launch (start us, length us, event | category | flops | bytes accessed | tf_op | source)
XLA Modules:
  0.0 566.2 jit_solution(11887050907164470776)
XLA Ops:
  0.6 543.0 %gradients.1 = (bf16[12,2,1024,1024]{3,2,1,0:T(8,128)(2,1)}, bf16[16,2048,1024]{2,1,0:T(8,128)(2,1)}, bf16[4,2048,1024]{2,1,0:T(8,128)(2,1)}, bf16[3,2048,1024]{...) custom-call(bf16[2048,1024]{1,0:T(8,128)(2,1)} %x_ref.1, bf16[2048,1024]{1,0:T(8,128)(2,1)} %t_ref.1, ...), custom_call_target="tpu_custom_call" | custom-call | tf_op jit(solution)/shard_map/gradients/pallas_call | solution.py:671
  543.7 0.0 copy-start
  543.7 12.8 %copy.8 = f32[4,1024,1024]{2,1,0:T(8,128)} copy(f32[4,1024,1024]{2,1,0:T(8,128)} %get-tuple-element.8) | data formatting | bytes 33554432
  556.5 3.6 copy-done
  560.1 6.2 %copy.9 = f32[4,1024,1024]{2,1,0:T(8,128)} copy(f32[4,1024,1024]{2,1,0:T(8,128)S(1)} %copy-done) | data formatting | bytes 33554432
Async XLA Ops:
  543.7 16.4 %copy-start = (f32[4,1024,1024]{2,1,0:T(8,128)S(1)}, f32[4,1024,1024]{2,1,0:T(8,128)}, u32[]{:S(2)}) copy-start(f32[4,1024,1024]{2,1,0:T(8,128)} %get-tuple-element.9) | copy-start | bytes 50331652
